TPU v7x, 256 devices: a whole 4x4x8 slice. The times are simulated.
256 devices in a mesh: var: 8 (over z), lat: 4 (over x), lon: 8 (over y, core).
Axes of the slice: x: 4, y: 4, z: 8, core: 2. Of those that a mesh axis runs over, the one named last changes fastest.
Arguments:
- state: bfloat16 [1, 256, 384, 1024], P(None, 'var', 'lat', 'lon'), may hold values from -6 to 6
- weights_in: bfloat16 [2, 256, 256], replicated, may hold values from -0.25 to 0.25
- bias_in: float32 [2, 256], replicated, may hold values from -3 to 3
- weights_out: bfloat16 [2, 256, 256], replicated, may hold values from -2 to 2
Outputs:
- field: bfloat16 [1, 256, 384, 1024], P(None, 'var', 'lat', 'lon')
- zonal: float32 [1, 256, 384], P(None, 'var', 'lat')
- energy: float32 [256], P('var')
All inputs are finite; a program needn't handle non-finite values.
Results may differ from a plain program's by a relative error of at most 0.012.
Values may be sent and summed in bfloat16 or wider, within the bound.
A program may use at most 64 MiB of HBM per device.

v0:
```python
import math

import jax
import jax.numpy as jnp
from jax import lax
from jax.sharding import PartitionSpec as P

LAT = 384
LON = 1024
MLAT = 96
MLON = 96


def split_up(shard, dim, peers):
    before, after = (shard.shape[:dim], shard.shape[dim + 1 :])
    return jnp.moveaxis(shard.reshape(*before, peers, -1, *after), dim, 0)


def sent_and_summed(shard, axis, dim):
    tiles = split_up(shard, dim, lax.axis_size(axis))
    arrived = lax.all_to_all(tiles, axis, split_axis=0, concat_axis=0, tiled=True)
    return arrived.sum(axis=0)


def in_order(tiles, dim):
    lengths = list(tiles.shape[1:])
    lengths[dim] *= tiles.shape[0]
    return jnp.moveaxis(tiles, 0, dim).reshape(lengths)


def from_everyone(shard, axis):
    peers = lax.axis_size(axis)
    return lax.all_to_all(
        jnp.broadcast_to(shard[None], (peers, *shard.shape)), axis, 0, 0, tiled=True
    )


def gathered_copies(shard, axis, dim):
    return in_order(from_everyone(shard, axis), dim)


def taken_together(shard, axis):
    everything = from_everyone(shard, axis)
    return jnp.sum(everything, axis=0)


def packed_total(arrays, axis):
    ravelled, at, done = (jnp.concatenate([a.reshape(-1) for a in arrays]), 0, [])
    so_far = taken_together(ravelled, axis)
    for a in arrays:
        done.append(so_far[at : at + a.size].reshape(a.shape))
        at += a.size
    return tuple(done)


def lon_forward(count):
    index = jnp.arange(count, dtype=jnp.int32)
    modes = jnp.arange(MLON, dtype=jnp.int32)
    phase = index[:, None] * modes[None, :] % LON
    angle = phase.astype(jnp.float32) * (2.0 * math.pi / LON)
    scale = 1.0 / math.sqrt(LAT * LON)
    return (jnp.stack([jnp.cos(angle), -jnp.sin(angle)], 1) * scale).astype(jnp.bfloat16)


def lat_forward(first, count):
    freqs = jnp.arange(MLAT, dtype=jnp.int32) - MLAT // 2
    index = first + jnp.arange(count, dtype=jnp.int32)
    phase = jnp.mod(freqs[:, None] * index[None, :], LAT)
    angle = phase.astype(jnp.float32) * (2.0 * math.pi / LAT)
    cosine, sine = (jnp.cos(angle), jnp.sin(angle))
    return jnp.stack([jnp.stack([cosine, sine]), jnp.stack([-sine, cosine])])


def lat_inverse(first, count):
    freqs = jnp.arange(MLAT, dtype=jnp.int32) - MLAT // 2
    index = first + jnp.arange(count, dtype=jnp.int32)
    phase = jnp.mod(index[:, None] * freqs[None, :], LAT)
    angle = phase.astype(jnp.float32) * (2.0 * math.pi / LAT)
    cosine, sine = (jnp.cos(angle), jnp.sin(angle))
    return jnp.stack([jnp.stack([cosine, -sine]), jnp.stack([sine, cosine])]).astype(jnp.bfloat16)


def lon_inverse(first, count):
    modes = jnp.arange(MLON, dtype=jnp.int32)
    index = first + jnp.arange(count, dtype=jnp.int32)
    phase = modes[:, None] * index[None, :] % LON
    angle = phase.astype(jnp.float32) * (2.0 * math.pi / LON)
    factor = jnp.where(modes == 0, 1.0, 2.0).astype(jnp.float32)[:, None] / math.sqrt(LAT * LON)
    return jnp.stack([factor * jnp.cos(angle), -factor * jnp.sin(angle)]).astype(jnp.bfloat16)


def area_weights(first, count):
    index = first + jnp.arange(count, dtype=jnp.int32)
    return jnp.cos(math.pi * ((index.astype(jnp.float32) + 0.5) / LAT - 0.5))


def complex_block(pair):
    real_part, imag_part = (pair[0], pair[1])
    return jnp.stack(
        [jnp.stack([real_part, -imag_part], 1), jnp.stack([imag_part, real_part], 1)], 0
    )


def body(state, weights_in, bias_in, weights_out):
    batch, cdev, latdev, londev = state.shape
    nlat = lax.axis_size("lat")
    nlon = lax.axis_size("lon")
    lat_first = lax.axis_index("lat") * latdev
    lon_first = lax.axis_index("lon") * londev
    modes_lat = MLAT // nlat
    modes_lon = MLON // nlon
    qtab = lat_forward(lat_first, latdev)
    qsplit = qtab.reshape(2, 2, nlat, modes_lat, latdev)
    columns = lax.all_to_all(state, "lon", split_axis=1, concat_axis=3, tiled=True)
    lonfull = jnp.einsum(
        "bcnl,lpk->pbcnk", columns, lon_forward(LON), preferred_element_type=jnp.float32
    )
    lonspec = lax.all_to_all(
        lonfull.astype(jnp.bfloat16), "lon", split_axis=4, concat_axis=2, tiled=True
    ).astype(lonfull.dtype)
    partial_value = jnp.einsum(
        "qpIJn,pbcnk->qbcIJk", qsplit, lonspec, precision=lax.Precision.HIGHEST
    )
    spectrum = sent_and_summed(partial_value.reshape(2, batch, cdev, -1), "lat", 3)
    spectrum = spectrum.astype(jnp.bfloat16)
    block_in = complex_block(weights_in)
    block_out = complex_block(weights_out)
    whole = gathered_copies(spectrum, "var", 2)
    owned = lax.dynamic_slice_in_dim(block_out, lax.axis_index("var") * cdev, cdev, 1)
    hidden = jnp.einsum("qhpc,pbcj->qbhj", block_in, whole, preferred_element_type=jnp.float32)
    hidden = jnp.maximum(hidden + bias_in[:, None, :, None], 0.0).astype(jnp.bfloat16)
    mixed = jnp.einsum("qoph,pbhj->qboj", owned, hidden, preferred_element_type=jnp.float32).astype(
        jnp.bfloat16
    )
    mixed = mixed.reshape(2, batch, cdev, modes_lat, modes_lon)
    rtab = lat_inverse(lat_first, latdev)
    table = rtab
    latback = jnp.einsum(
        "qpnj,pbcjk->qbcnk",
        table,
        gathered_copies(mixed, "lat", 3),
        preferred_element_type=jnp.float32,
    ).astype(jnp.bfloat16)
    htab = lon_inverse(lon_first, londev)
    table = htab
    result = jnp.einsum(
        "pbcnk,pkl->bcnl",
        gathered_copies(latback, "lon", 4),
        table,
        preferred_element_type=jnp.float32,
    )
    active = jax.nn.gelu(result, approximate=False)
    field = active.astype(jnp.bfloat16)
    weights = area_weights(lat_first, latdev)
    denominator = batch * LON * jnp.sum(area_weights(0, LAT))
    row_total = jnp.sum(active, -1)
    row_square = jnp.sum(active * active, -1)
    summed, squared = packed_total((row_total, row_square), "lon")
    zonal = summed / LON
    local = jnp.sum(squared * weights[None, None, :], axis=(0, 2))
    energy = taken_together(local, "lat") / denominator
    return (field, zonal, energy)


def solution(mesh):
    return jax.shard_map(
        body,
        mesh=mesh,
        in_specs=(P(None, "var", "lat", "lon"), P(), P(), P()),
        out_specs=(P(None, "var", "lat", "lon"), P(None, "var", "lat"), P("var")),
        check_vma=False,
    )
```

profile of v0, /device:TPU:1, one launch (start us, length us, event | category | flops | bytes accessed | tf_op | source)
XLA Modules:
  0.0 134.0 jit_solution(15491810262446491308)
XLA Ops:
  0.7 6.8 %all-to-all-start = ((bf16[1,32,96,128]{3,2,0,1:T(8,128)(2,1)}), bf16[1,32,96,128]{3,2,0,1:T(8,128)(2,1)S(1)}, u32[]{:S(2)}, u32[]{:S(2)}) async-start(bf16[1,32,96,128]{3,2,0,1:T(8,128)(2,1)} %bitcast.197), calls=%async_computation | async-start | bytes 1572864 | tf_op jit(solution)/shard_map/all_to_all | solution.py:114
  7.5 1.6 %sine_negate_fusion = (f32[1024,1,96]{0,2,1:T(8,128)S(1)}, f32[1024,1,96]{0,2,1:T(8,128)S(1)}) fusion(), kind=kLoop, calls=%fused_computation.57 | loop fusion | flops 1474560 | bytes 786432 | tf_op jit(solution)/shard_map/neg | solution.py:62
  9.1 10.5 %all-to-all-done = bf16[1,32,96,128]{3,2,0,1:T(8,128)(2,1)S(1)} async-done(((bf16[1,32,96,128]{3,2,0,1:T(8,128)(2,1)}), bf16[1,32,96,128]{3,2,0,1:T(8,128)(2,1)S(1)}, u32[]{:S(2)}, u32[]{:S(2)}) %all-to-all-start) | async-done | bytes 786464 | tf_op jit(solution)/shard_map/all_to_all | solution.py:114
  19.6 0.5 copy.120
  20.1 0.3 reshape.794
  20.5 0.5 fusion.23
  20.9 0.8 copy.79
  21.7 4.3 %all-to-all-start.1 = ((bf16[2,1,4,96,96]{3,2,0,1,4:T(4,128)(2,1)}), bf16[2,1,4,96,96]{3,2,0,1,4:T(4,128)(2,1)S(1)}, u32[]{:S(2)}, u32[]{:S(2)}) async-start(bf16[2,1,4,96,96]{3,2,0,1,4:T(4,128)(2,1)} %copy.79), calls=%async_computation.1 | async-start | bytes 393216 | tf_op jit(solution)/shard_map/all_to_all | solution.py:118
  26.0 0.3 fusion.75
  26.3 5.6 %all-to-all-done.1 = bf16[2,1,4,96,96]{3,2,0,1,4:T(4,128)(2,1)S(1)} async-done(((bf16[2,1,4,96,96]{3,2,0,1,4:T(4,128)(2,1)}), bf16[2,1,4,96,96]{3,2,0,1,4:T(4,128)(2,1)S(1)}, u32[]{:S(2)}, u32[]{:S(2)}) %all-to-all-start.1) | async-done | bytes 147488 | tf_op jit(solution)/shard_map/all_to_all | solution.py:118
  31.9 0.1 copy.81
  32.0 0.6 convolution_bitcast_fusion
  32.7 0.3 copy.82
  33.0 1.2 copy.83
  34.2 3.5 %all-to-all-start.2 = ((f32[4,2,1,32,288]{4,3,2,1,0:T(8,128)}), f32[4,2,1,32,288]{4,3,2,1,0:T(8,128)S(1)}, u32[]{:S(2)}, u32[]{:S(2)}) async-start(f32[4,2,1,32,288]{4,3,2,1,0:T(8,128)} %copy.83), calls=%async_computation.2 | async-start | bytes 786432 | tf_op jit(solution)/shard_map/all_to_all | solution.py:21
  37.7 6.7 %all-to-all-done.2 = f32[4,2,1,32,288]{4,3,2,1,0:T(8,128)S(1)} async-done(((f32[4,2,1,32,288]{4,3,2,1,0:T(8,128)}), f32[4,2,1,32,288]{4,3,2,1,0:T(8,128)S(1)}, u32[]{:S(2)}, u32[]{:S(2)}) %all-to-all-start.2) | async-done | bytes 294944 | tf_op jit(solution)/shard_map/all_to_all | solution.py:21
  44.4 0.8 broadcast_in_dim.22
  45.2 7.9 %all-to-all-start.3 = ((bf16[8,2,1,32,288]{4,3,1,2,0:T(8,128)(2,1)}), bf16[8,2,1,32,288]{4,3,1,2,0:T(8,128)(2,1)S(1)}, u32[]{:S(2)}, u32[]{:S(2)}) async-start(bf16[8,2,1,32,288]{4,3,1,2,0:T(8,128)(2,1)} %broadcast_in_dim.22), calls=%async_computation.3 | async-start | bytes 786432 | tf_op jit(solution)/shard_map/all_to_all | solution.py:33
  53.2 0.1 maximum_bitcast_fusion
  53.3 0.3 negate_convert_fusion
  53.6 11.3 %all-to-all-done.3 = bf16[8,2,1,32,288]{4,3,1,2,0:T(8,128)(2,1)S(1)} async-done(((bf16[8,2,1,32,288]{4,3,1,2,0:T(8,128)(2,1)}), bf16[8,2,1,32,288]{4,3,1,2,0:T(8,128)(2,1)S(1)}, u32[]{:S(2)}, u32[]{:S(2)}) %all-to-all-start.3) | async-done | bytes 294944 | tf_op jit(solution)/shard_map/all_to_all | solution.py:33
  64.9 0.6 fusion.27
  65.5 0.2 copy.88
  65.7 0.1 broadcast_bitcast_fusion
  65.8 1.2 reshape.810
  67.0 3.3 %all-to-all-start.4 = ((bf16[4,2,9216]{2,1,0:T(2,128)(2,1)}), bf16[4,2,9216]{2,1,0:T(2,128)(2,1)S(1)}, u32[]{:S(2)}, u32[]{:S(2)}) async-start(bf16[4,2,9216]{2,1,0:T(2,128)(2,1)} %reshape.810), calls=%async_computation.4 | async-start | bytes 294912 | tf_op jit(solution)/shard_map/all_to_all | solution.py:33
  70.4 4.8 %all-to-all-done.4 = bf16[4,2,9216]{2,1,0:T(2,128)(2,1)S(1)} async-done(((bf16[4,2,9216]{2,1,0:T(2,128)(2,1)}), bf16[4,2,9216]{2,1,0:T(2,128)(2,1)S(1)}, u32[]{:S(2)}, u32[]{:S(2)}) %all-to-all-start.4) | async-done | bytes 147488 | tf_op jit(solution)/shard_map/all_to_all | solution.py:33
  75.2 0.3 reshape.811
  75.6 0.6 copy.107
  76.2 0.4 reshape.802
  76.6 0.2 fusion.24
  76.9 1.5 %broadcast_in_dim.26 = bf16[8,2,1,32,96,12]{4,3,5,1,2,0:T(8,128)(2,1)} broadcast(bf16[2,32,96,12]{2,1,3,0:T(8,128)(2,1)S(1)} %copy.92), dimensions={1,3,4,5} | broadcast | bytes 1327104 | tf_op jit(solution)/shard_map/broadcast_in_dim | solution.py:34
  78.3 8.5 %all-to-all-start.5 = ((bf16[8,2,1,32,96,12]{4,3,5,1,2,0:T(8,128)(2,1)}), bf16[8,2,1,32,96,12]{4,3,5,1,2,0:T(8,128)(2,1)S(1)}, u32[]{:S(2)}, u32[]{:S(2)}) async-start(bf16[8,2,1,32,96,12]{4,3,5,1,2,0:T(8,128)(2,1)} %broadcast_in_dim.26), calls=%async_computation.5 | async-start | bytes 3145728 | tf_op jit(solution)/shard_map/all_to_all | solution.py:33
  86.9 0.2 multiply_convert_fusion.1
  87.1 20.4 %all-to-all-done.5 = bf16[8,2,1,32,96,12]{4,3,5,1,2,0:T(8,128)(2,1)S(1)} async-done(((bf16[8,2,1,32,96,12]{4,3,5,1,2,0:T(8,128)(2,1)}), bf16[8,2,1,32,96,12]{4,3,5,1,2,0:T(8,128)(2,1)S(1)}, u32[]{:S(2)}, u32[]{:S(2)}) %all-to-all-start.5) | async-done | bytes 1179680 | tf_op jit(solution)/shard_map/all_to_all | solution.py:33
  107.5 0.3 copy.93
  107.8 6.6 %fusion.94 = (f32[32,96]{1,0:T(8,128)S(1)}, f32[32,96]{1,0:T(8,128)S(1)}, bf16[1,32,96,128]{3,2,1,0:T(8,128)(2,1)}) fusion(bf16[1,96,128]{2,1,0:T(8,128)(2,1)S(1)} %get-tuple-element.25, bf16[1,96,128]{2,1,0:T(8,128)(2,1)S(1)} %get-tuple-element.24, bf16[2,32,96,96]{2,1,3,0:T(8,128)(2,1)S(1)} %bitcast.194), kind=kOutput, calls=%fused_computation.144 | convolution fusion | flops 177752064 | bytes 2039808 | tf_op jit(solution)/shard_map/pbcnk,pkl->bcnl/dot_general | solution.py:146
  114.5 0.8 broadcast_in_dim.29
  115.3 4.3 %all-to-all-start.6 = ((f32[8,1,6144]{2,1,0:T(1,128)}), f32[8,1,6144]{2,1,0:T(1,128)S(1)}, u32[]{:S(2)}, u32[]{:S(2)}) async-start(f32[8,1,6144]{2,1,0:T(1,128)} %broadcast_in_dim.29), calls=%async_computation.6 | async-start | bytes 393216 | tf_op jit(solution)/shard_map/all_to_all | solution.py:33
  119.6 5.8 %all-to-all-done.6 = f32[8,1,6144]{2,1,0:T(1,128)S(1)} async-done(((f32[8,1,6144]{2,1,0:T(1,128)}), f32[8,1,6144]{2,1,0:T(1,128)S(1)}, u32[]{:S(2)}, u32[]{:S(2)}) %all-to-all-start.6) | async-done | bytes 196640 | tf_op jit(solution)/shard_map/all_to_all | solution.py:33
  125.4 0.1 reduce_sum.66
  125.6 0.1 multiply_reduce_fusion.1
  125.8 0.6 broadcast_in_dim.30
  126.4 3.2 %all-to-all-start.7 = ((f32[4,1,32]{2,1,0:T(1,128)}), f32[4,1,32]{2,1,0:T(1,128)S(1)}, u32[]{:S(2)}, u32[]{:S(2)}) async-start(f32[4,1,32]{2,1,0:T(1,128)} %broadcast_in_dim.30), calls=%async_computation.7 | async-start | bytes 4096 | tf_op jit(solution)/shard_map/all_to_all | solution.py:33
  129.5 0.6 cosine_reduce_fusion
  130.8 0.7 div.38
  131.5 2.0 %all-to-all-done.7 = f32[4,1,32]{2,1,0:T(1,128)S(1)} async-done(((f32[4,1,32]{2,1,0:T(1,128)}), f32[4,1,32]{2,1,0:T(1,128)S(1)}, u32[]{:S(2)}, u32[]{:S(2)}) %all-to-all-start.7) | async-done | bytes 544 | tf_op jit(solution)/shard_map/all_to_all | solution.py:33
  133.5 0.5 broadcast_divide_fusion
  (28 shorter events, 0.6 us)
Async XLA Ops:
  0.6 8.4 %copy-start.1 = (bf16[2,256,256]{2,1,0:T(8,128)(2,1)S(1)}, bf16[2,256,256]{2,1,0:T(8,128)(2,1)}, u32[]{:S(2)}) copy-start(bf16[2,256,256]{2,1,0:T(8,128)(2,1)} %param.7) | copy-start | bytes 786436
  0.6 8.4 %copy-start = (bf16[2,256,256]{2,1,0:T(8,128)(2,1)S(1)}, bf16[2,256,256]{2,1,0:T(8,128)(2,1)}, u32[]{:S(2)}) copy-start(bf16[2,256,256]{2,1,0:T(8,128)(2,1)} %param.5) | copy-start | bytes 786436
  0.7 19.0 %all-to-all-start = ((bf16[1,32,96,128]{3,2,0,1:T(8,128)(2,1)}), bf16[1,32,96,128]{3,2,0,1:T(8,128)(2,1)S(1)}, u32[]{:S(2)}, u32[]{:S(2)}) async-start(bf16[1,32,96,128]{3,2,0,1:T(8,128)(2,1)} %bitcast.197), calls=%async_computation | async-start | bytes 1572864 | tf_op jit(solution)/shard_map/all_to_all | solution.py:114
  21.7 10.1 %all-to-all-start.1 = ((bf16[2,1,4,96,96]{3,2,0,1,4:T(4,128)(2,1)}), bf16[2,1,4,96,96]{3,2,0,1,4:T(4,128)(2,1)S(1)}, u32[]{:S(2)}, u32[]{:S(2)}) async-start(bf16[2,1,4,96,96]{3,2,0,1,4:T(4,128)(2,1)} %copy.79), calls=%async_computation.1 | async-start | bytes 393216 | tf_op jit(solution)/shard_map/all_to_all | solution.py:118
  34.2 10.2 %all-to-all-start.2 = ((f32[4,2,1,32,288]{4,3,2,1,0:T(8,128)}), f32[4,2,1,32,288]{4,3,2,1,0:T(8,128)S(1)}, u32[]{:S(2)}, u32[]{:S(2)}) async-start(f32[4,2,1,32,288]{4,3,2,1,0:T(8,128)} %copy.83), calls=%async_computation.2 | async-start | bytes 786432 | tf_op jit(solution)/shard_map/all_to_all | solution.py:21
  45.2 19.7 %all-to-all-start.3 = ((bf16[8,2,1,32,288]{4,3,1,2,0:T(8,128)(2,1)}), bf16[8,2,1,32,288]{4,3,1,2,0:T(8,128)(2,1)S(1)}, u32[]{:S(2)}, u32[]{:S(2)}) async-start(bf16[8,2,1,32,288]{4,3,1,2,0:T(8,128)(2,1)} %broadcast_in_dim.22), calls=%async_computation.3 | async-start | bytes 786432 | tf_op jit(solution)/shard_map/all_to_all | solution.py:33
  53.1 11.8 %copy-start.2 = (f32[2,256]{1,0:T(2,128)S(1)}, f32[2,256]{1,0:T(2,128)}, u32[]{:S(2)}) copy-start(f32[2,256]{1,0:T(2,128)} %param.6) | copy-start | bytes 6148
  67.0 8.2 %all-to-all-start.4 = ((bf16[4,2,9216]{2,1,0:T(2,128)(2,1)}), bf16[4,2,9216]{2,1,0:T(2,128)(2,1)S(1)}, u32[]{:S(2)}, u32[]{:S(2)}) async-start(bf16[4,2,9216]{2,1,0:T(2,128)(2,1)} %reshape.810), calls=%async_computation.4 | async-start | bytes 294912 | tf_op jit(solution)/shard_map/all_to_all | solution.py:33
  78.3 29.2 %all-to-all-start.5 = ((bf16[8,2,1,32,96,12]{4,3,5,1,2,0:T(8,128)(2,1)}), bf16[8,2,1,32,96,12]{4,3,5,1,2,0:T(8,128)(2,1)S(1)}, u32[]{:S(2)}, u32[]{:S(2)}) async-start(bf16[8,2,1,32,96,12]{4,3,5,1,2,0:T(8,128)(2,1)} %broadcast_in_dim.26), calls=%async_computation.5 | async-start | bytes 3145728 | tf_op jit(solution)/shard_map/all_to_all | solution.py:33
  115.3 10.1 %all-to-all-start.6 = ((f32[8,1,6144]{2,1,0:T(1,128)}), f32[8,1,6144]{2,1,0:T(1,128)S(1)}, u32[]{:S(2)}, u32[]{:S(2)}) async-start(f32[8,1,6144]{2,1,0:T(1,128)} %broadcast_in_dim.29), calls=%async_computation.6 | async-start | bytes 393216 | tf_op jit(solution)/shard_map/all_to_all | solution.py:33
  126.4 7.1 %all-to-all-start.7 = ((f32[4,1,32]{2,1,0:T(1,128)}), f32[4,1,32]{2,1,0:T(1,128)S(1)}, u32[]{:S(2)}, u32[]{:S(2)}) async-start(f32[4,1,32]{2,1,0:T(1,128)} %broadcast_in_dim.30), calls=%async_computation.7 | async-start | bytes 4096 | tf_op jit(solution)/shard_map/all_to_all | solution.py:33
where the time goes:
time: 135 us; the launch traced here: 134 us
  waiting for transfers between devices  67.2 us (50%)
  starting transfers between devices  41.8 us (31%)
  local copies, waits for them, and re-layouts  11 us (8%)
  matrix products  8.46 us (6%)
  other arithmetic  4.04 us (3%)
  between operations  1.58 us (1%)
    all_to_all x5, waiting for transfers between devices, from_everyone(): lax.all_to_all(jnp.broadcast_to(shard[None], (peers, *shard.shape)), axis...  44.3 us
    all_to_all x5, starting transfers between devices, from_everyone(): lax.all_to_all(jnp.broadcast_to(shard[None], (peers, *shard.shape)), axis...  27.2 us
    all_to_all x1, waiting for transfers between devices, body(): lax.all_to_all(state, 'lon', split_axis=1, concat_axis=3, tiled=True)  10.5 us
    all_to_all x1, starting transfers between devices, body(): lax.all_to_all(state, 'lon', split_axis=1, concat_axis=3, tiled=True)  6.79 us
    all_to_all x1, waiting for transfers between devices, sent_and_summed(): lax.all_to_all(tiles, axis, split_axis=0, concat_axis=0, tiled=True)  6.72 us
    dot_general x1, matrix products, body(): jnp.einsum('pbcnk,pkl->bcnl', gathered_copies(latback, 'lon', 4), table,...  6.56 us
    all_to_all x1, waiting for transfers between devices, body(): lax.all_to_all(lonfull.astype(jnp.bfloat16), 'lon', split_axis=4, concat_...  5.6 us
    all_to_all x1, starting transfers between devices, body(): lax.all_to_all(lonfull.astype(jnp.bfloat16), 'lon', split_axis=4, concat_...  4.25 us
  transfers between devices with their start and end apart: 8, of which 8 were waited for; matrix products, arithmetic and copies ran while one was open for 3% of the time, Pallas kernels for 0%

commit v1 on v0

v1 whole, which is shorter than its diff:
```python
import math

import jax
import jax.numpy as jnp
import numpy as np
from jax import lax
from jax.experimental import pallas as pl
from jax.experimental.pallas import tpu as pltpu
from jax.sharding import PartitionSpec as P

LAT = 384
LON = 1024
MLAT = 96
MLON = 96
NVAR = 8
NLAT = 4
NLON = 8
PLANE = NLAT * NLON
CD = 32
RD = LAT // NLAT
ND = LON // NLON
JO = MLAT // PLANE
MESH = pl.DeviceIdType.MESH
BF = jnp.bfloat16
F32 = jnp.float32


def tables():
    k = np.arange(MLON)
    n = np.arange(LON)
    angle = 2.0 * np.pi / LON * ((n[:, None] * k[None, :]) % LON)
    scale = 1.0 / math.sqrt(LAT * LON)
    etab = np.zeros((LON, 256), np.float32)
    etab[:, :MLON] = np.cos(angle) * scale
    etab[:, 128 : 128 + MLON] = -np.sin(angle) * scale
    weight = np.where(k == 0, 1.0, 2.0)[:, None] * scale
    full = np.zeros((256, LON), np.float32)
    full[:MLON] = weight * np.cos(angle.T)
    full[128 : 128 + MLON] = -weight * np.sin(angle.T)
    htab = full.reshape(256, NLON, ND).transpose(1, 0, 2)
    r = np.arange(LAT)
    freqs = np.arange(MLAT) - MLAT // 2
    turn = 2.0 * np.pi / LAT * np.mod(freqs[:, None] * r[None, :], LAT)
    cosine, sine = np.cos(turn), np.sin(turn)
    forward = np.zeros((PLANE, 8, 2, LAT), np.float32)
    forward[:, 0:3, 0] = cosine.reshape(PLANE, JO, LAT)
    forward[:, 0:3, 1] = sine.reshape(PLANE, JO, LAT)
    forward[:, 3:6, 0] = -sine.reshape(PLANE, JO, LAT)
    forward[:, 3:6, 1] = cosine.reshape(PLANE, JO, LAT)
    qtab = forward.reshape(PLANE * 8, 2 * LAT)
    rtab = qtab.T
    area = np.cos(np.pi * ((r + 0.5) / LAT - 0.5))
    gtab = np.broadcast_to(area.reshape(NLAT, 1, RD), (NLAT, 8, RD))
    bf = lambda t: np.ascontiguousarray(t).astype(jnp.bfloat16)
    return (
        bf(etab),
        bf(qtab),
        bf(rtab),
        bf(htab),
        np.ascontiguousarray(gtab).astype(np.float32),
        float(LON * area.sum()),
    )


def kernel(
    total_area,
    state,
    etab,
    qtab,
    rtab,
    htab,
    gtab,
    win,
    bias,
    wout,
    field,
    zonal,
    energy,
    st,
    ev,
    qv,
    rv,
    hv,
    gv,
    wiv,
    wov,
    bcol,
    xin,
    lv,
    sbuf,
    srecv,
    xf,
    xall,
    mf,
    mbuf,
    mrecv,
    lbv,
    fs,
    zst,
    strec,
    load_sem,
    s1,
    r1,
    s2,
    r2,
    s3,
    r3,
    s4,
    r4,
    s5,
    r5,
    s6,
    r6,
):
    v = lax.axis_index("var")
    a = lax.axis_index("lat")
    b = lax.axis_index("lon")
    me = a * NLON + b
    y, core = lax.div(b, 2), lax.rem(b, 2)

    def plane(d):
        part = lax.rem(d, 8)
        pa = lax.rem(a + lax.div(d, 8), NLAT)
        py = lax.rem(y + lax.div(part, 2), 4)
        pc = lax.rem(core + part, 2)
        return pa, py * 2 + pc

    loads = [
        pltpu.make_async_copy(src, dst, load_sem.at[i])
        for i, (src, dst) in enumerate(
            [
                (state.at[0], st),
                (etab, ev),
                (qtab, qv),
                (win, wiv),
                (wout, wov),
                (rtab, rv),
                (htab, hv),
                (gtab, gv),
            ]
        )
    ]
    for load in loads:
        load.start()

    barrier = pltpu.get_barrier_semaphore()

    def greet(d, _):
        pa, pb = plane(d)
        pl.semaphore_signal(barrier, inc=1, device_id={"lat": pa, "lon": pb}, device_id_type=MESH)
        return 0

    lax.fori_loop(1, PLANE, greet, 0)

    def greet_var(d, _):
        pv = lax.rem(v + d, NVAR)
        pl.semaphore_signal(barrier, inc=1, device_id={"var": pv}, device_id_type=MESH)
        return 0

    lax.fori_loop(1, NVAR, greet_var, 0)
    bcol[...] = jnp.zeros_like(bcol)
    bcol[0:2, :] = bias[...]
    turned = jnp.transpose(bcol[...])
    bias_r = jnp.broadcast_to(turned[:, 0:1], (256, 128))
    bias_i = jnp.broadcast_to(turned[:, 1:2], (256, 128))
    mf[...] = jnp.zeros_like(mf)
    zst[...] = jnp.zeros_like(zst)
    loads[0].wait()
    pl.semaphore_wait(barrier, PLANE - 1 + NVAR - 1)

    def send1(d, _):
        pa, pb = plane(d)
        pltpu.make_async_remote_copy(
            src_ref=st.at[pa * NLON + pb],
            dst_ref=xin.at[me],
            send_sem=s1.at[d],
            recv_sem=r1.at[me],
            device_id={"lat": pa, "lon": pb},
            device_id_type=MESH,
        ).start()
        return 0

    lax.fori_loop(1, PLANE, send1, 0)
    xin[me] = st[me]

    def copy1(d, slot, pa, pb):
        return pltpu.make_async_remote_copy(
            src_ref=st.at[slot],
            dst_ref=xin.at[slot],
            send_sem=s1.at[d],
            recv_sem=r1.at[slot],
            device_id={"lat": pa, "lon": pb},
            device_id_type=MESH,
        )

    loads[1].wait()
    for da in range(NLAT):

        def wait1(d, _):
            pa, pb = plane(d)
            copy1(d, pa * NLON + pb, pa, pb).wait_recv()
            return 0

        lax.fori_loop(max(1, da * 8), da * 8 + 8, wait1, 0)
        pa = lax.rem(a + da, NLAT)
        rows = jnp.concatenate([xin[pa * NLON + i] for i in range(NLON)], axis=1)
        lv[pa] = jnp.dot(rows, ev[...], preferred_element_type=F32).astype(BF)

    loads[2].wait()
    lon = lv[...].reshape(LAT, 256)
    spec = jnp.dot(qv[:, 0:LAT], lon[:, 0:128], preferred_element_type=F32)
    spec += jnp.dot(qv[:, LAT : 2 * LAT], lon[:, 128:256], preferred_element_type=F32)
    sbuf[...] = spec.reshape(PLANE, 8, 128).astype(BF)

    def copy2(d, src, dst, pa, pb):
        return pltpu.make_async_remote_copy(
            src_ref=sbuf.at[src],
            dst_ref=srecv.at[dst],
            send_sem=s2.at[d],
            recv_sem=r2.at[dst],
            device_id={"lat": pa, "lon": pb},
            device_id_type=MESH,
        )

    def send2(d, _):
        pa, pb = plane(d)
        copy2(d, pa * NLON + pb, me, pa, pb).start()
        return 0

    lax.fori_loop(1, PLANE, send2, 0)
    srecv[me] = sbuf[me]

    def wait2(d, _):
        pa, pb = plane(d)
        slot = pa * NLON + pb
        copy2(d, slot, slot, pa, pb).wait_recv()
        return 0

    lax.fori_loop(1, PLANE, wait2, 0)
    xf[...] = srecv[...].astype(F32).reshape(PLANE * 8, 128)
    t = [xf[pl.ds(i, PLANE, stride=8), :] for i in range(6)]
    lane = lax.broadcasted_iota(jnp.int32, (PLANE, 128), 1)
    low, high = lane < 32, lane >= 96

    def packed(t0, t1, t2):
        up, half = pltpu.roll(t2, 96, 1), pltpu.roll(t2, 64, 1)
        return jnp.where(high, up, t0), jnp.where(high, half, t1), up, half

    p0, p1, _, last_r = packed(*t[0:3])
    p2, p3, last_i, _ = packed(*t[3:6])
    second = jnp.logical_and(lane >= 32, lane < 64)
    p4 = jnp.where(low, last_r, jnp.where(second, last_i, 0.0))
    xall[v] = jnp.concatenate([p0, p1, p2, p3, p4], axis=1).astype(BF)

    def copy3(d, slot):
        pv = lax.rem(v + d, NVAR)
        return pltpu.make_async_remote_copy(
            src_ref=xall.at[slot],
            dst_ref=xall.at[slot],
            send_sem=s3.at[d],
            recv_sem=r3.at[slot],
            device_id={"var": pv},
            device_id_type=MESH,
        )

    def send3(d, _):
        copy3(d, v).start()
        return 0

    lax.fori_loop(1, NVAR, send3, 0)

    def wait3(d, _):
        copy3(d, lax.rem(v + d, NVAR)).wait_recv()
        return 0

    loads[3].wait()
    loads[4].wait()
    lax.fori_loop(1, NVAR, wait3, 0)
    every = xall[...].reshape(NVAR * CD, 640)

    def combined(g, half):
        re = g[:half, 0:256] - g[half:, 256:512]
        im = g[half:, 0:256] + g[:half, 256:512]
        gr, gi = g[:half, 512:640], g[half:, 512:640]
        which = lax.broadcasted_iota(jnp.int32, (half, 128), 1) < 32
        last = jnp.where(which, gr - pltpu.roll(gi, 96, 1), gr + pltpu.roll(gi, 32, 1))
        return re, im, last, which

    g = jnp.dot(wiv[...].reshape(512, 256), every, preferred_element_type=F32)
    re, im, last, which = combined(g, 256)
    wide_r = jnp.concatenate([bias_r, bias_r], axis=1)
    wide_i = jnp.concatenate([bias_i, bias_i], axis=1)
    hidden = jnp.concatenate(
        [re + wide_r, im + wide_i, last + jnp.where(which, bias_r, bias_i)], axis=1
    )
    hidden = jnp.maximum(hidden, 0.0).astype(BF)
    first = pl.multiple_of(v * CD, CD)
    own = jnp.concatenate([wov[0, pl.ds(first, CD), :], wov[1, pl.ds(first, CD), :]], axis=0)
    g = jnp.dot(own, hidden, preferred_element_type=F32)
    re, im, last, _ = combined(g, CD)
    sel = [lane < 32, lane < 64]
    t2 = jnp.where(
        sel[0],
        pltpu.roll(re[:, 0:128], 32, 1),
        jnp.where(sel[1], pltpu.roll(re[:, 128:256], 64, 1), pltpu.roll(last, 64, 1)),
    )
    t5 = jnp.where(
        sel[0],
        pltpu.roll(im[:, 0:128], 32, 1),
        jnp.where(sel[1], pltpu.roll(im[:, 128:256], 64, 1), pltpu.roll(last, 32, 1)),
    )
    for i, tile in enumerate([re[:, 0:128], re[:, 128:256], t2, im[:, 0:128], im[:, 128:256], t5]):
        mf[pl.ds(i, PLANE, stride=8), :] = tile
    mbuf[...] = mf[...].reshape(PLANE, 8, 128).astype(BF)

    def copy4(d, src, dst, pa, pb):
        return pltpu.make_async_remote_copy(
            src_ref=mbuf.at[src],
            dst_ref=mrecv.at[dst],
            send_sem=s4.at[d],
            recv_sem=r4.at[dst],
            device_id={"lat": pa, "lon": pb},
            device_id_type=MESH,
        )

    def send4(d, _):
        pa, pb = plane(d)
        copy4(d, pa * NLON + pb, me, pa, pb).start()
        return 0

    lax.fori_loop(1, PLANE, send4, 0)
    mrecv[me] = mbuf[me]

    def wait4(d, _):
        pa, pb = plane(d)
        slot = pa * NLON + pb
        copy4(d, slot, slot, pa, pb).wait_recv()
        return 0

    for i in range(5, 8):
        loads[i].wait()
    lax.fori_loop(1, PLANE, wait4, 0)
    modes = mrecv[...].reshape(PLANE * 8, 128)
    back_r = jnp.dot(rv[0:LAT, :], modes, preferred_element_type=F32)
    back_i = jnp.dot(rv[LAT : 2 * LAT, :], modes, preferred_element_type=F32)
    lbv[...] = jnp.concatenate([back_r, back_i], axis=1).astype(BF).reshape(NLAT, RD, 256)

    def copy5(d, slot, pa, pb):
        return pltpu.make_async_remote_copy(
            src_ref=fs.at[d],
            dst_ref=field.at[0, slot],
            send_sem=s5.at[d],
            recv_sem=r5.at[slot],
            device_id={"lat": pa, "lon": pb},
            device_id_type=MESH,
        )

    def block(d):
        pa, pb = plane(d)
        out = jnp.dot(lbv[pa], hv[pb], preferred_element_type=F32)
        act = 0.5 * out * (1.0 + lax.erf(out * (1.0 / math.sqrt(2.0))))
        fs[d] = act.astype(BF)
        return act, pa, pb

    ones = jnp.ones((8, 128), F32)
    weighted = jnp.zeros((8, 128), F32)
    for da in reversed(range(NLAT)):

        def step(d, sums):
            act, pa, pb = block(d)
            copy5(d, me, pa, pb).start()
            return sums[0] + act, sums[1] + act * act

        zero = jnp.zeros((RD, 128), F32)
        if da:
            sums = (zero, zero)
        else:
            act, _, _ = block(0)
            kept = pltpu.make_async_copy(fs.at[0], field.at[0, me], s5.at[0])
            kept.start()
            sums = (act, act * act)
        sums = lax.fori_loop(max(1, da * 8), da * 8 + 8, step, sums)
        pa = lax.rem(a + da, NLAT)
        rowsum = lax.dot_general(
            ones,
            sums[0],
            (((1,), (1,)), ((), ())),
            precision=lax.Precision.HIGHEST,
            preferred_element_type=F32,
        )
        zst[pa, 0:1, 0:RD] = rowsum[0:1] * (1.0 / LON)
        weighted += jnp.dot(
            gv[pa], sums[1], precision=lax.Precision.HIGHEST, preferred_element_type=F32
        )
    total = jnp.sum(weighted, axis=1, keepdims=True)[0:1] * (1.0 / total_area)
    mine = jnp.where(lax.broadcasted_iota(jnp.int32, (1, 128), 1) == me, total, 0.0)
    for band in range(NLAT):
        zst[band, 1:2, :] = mine

    def copy6(d, slot, pa, pb):
        return pltpu.make_async_remote_copy(
            src_ref=zst.at[pa],
            dst_ref=strec.at[slot],
            send_sem=s6.at[d],
            recv_sem=r6.at[slot],
            device_id={"lat": pa, "lon": pb},
            device_id_type=MESH,
        )

    def send6(d, _):
        pa, pb = plane(d)
        copy6(d, me, pa, pb).start()
        return 0

    lax.fori_loop(1, PLANE, send6, 0)
    strec[me] = zst[a]

    def wait6(d, _):
        pa, pb = plane(d)
        copy6(d, pa * NLON + pb, pa, pb).wait_recv()
        return 0

    lax.fori_loop(1, PLANE, wait6, 0)
    gathered = jnp.zeros((1, 128), F32)
    for i in range(CD):
        both = strec[i]
        zonal[i : i + 1, :] = both[0:1, 0:RD]
        gathered += both[1:2, :]
    energy[...] = gathered

    def drain(d, _):
        pa, pb = plane(d)
        slot = pa * NLON + pb
        copy5(d, slot, pa, pb).wait_recv()
        copy1(d, slot, pa, pb).wait_send()
        copy2(d, slot, slot, pa, pb).wait_send()
        copy4(d, slot, slot, pa, pb).wait_send()
        copy5(d, slot, pa, pb).wait_send()
        copy6(d, slot, pa, pb).wait_send()
        return 0

    lax.fori_loop(1, PLANE, drain, 0)

    def drain3(d, _):
        copy3(d, v).wait_send()
        return 0

    lax.fori_loop(1, NVAR, drain3, 0)
    kept.wait()


def body(state, weights_in, bias_in, weights_out):
    *tabs, total_area = tables()
    hbm = pl.BlockSpec(memory_space=pltpu.HBM)
    vmem = pl.BlockSpec(memory_space=pltpu.VMEM)
    dma = pltpu.SemaphoreType.DMA
    field, zonal, energy = pl.pallas_call(
        lambda *refs: kernel(total_area, *refs),
        out_shape=(
            jax.ShapeDtypeStruct((1, CD, RD, ND), BF),
            jax.ShapeDtypeStruct((CD, RD), F32),
            jax.ShapeDtypeStruct((1, 128), F32),
        ),
        in_specs=[hbm] * 7 + [vmem, hbm],
        out_specs=(hbm, vmem, vmem),
        scratch_shapes=[
            pltpu.VMEM((CD, RD, ND), BF),
            pltpu.VMEM((LON, 256), BF),
            pltpu.VMEM((256, 2 * LAT), BF),
            pltpu.VMEM((2 * LAT, 256), BF),
            pltpu.VMEM((NLON, 256, ND), BF),
            pltpu.VMEM((NLAT, 8, RD), F32),
            pltpu.VMEM((2, 256, 256), BF),
            pltpu.VMEM((2, 256, 256), BF),
            pltpu.VMEM((128, 256), F32),
            pltpu.VMEM((PLANE, RD, ND), BF),
            pltpu.VMEM((NLAT, RD, 256), BF),
            pltpu.VMEM((PLANE, 8, 128), BF),
            pltpu.VMEM((PLANE, 8, 128), BF),
            pltpu.VMEM((PLANE * 8, 128), F32),
            pltpu.VMEM((NVAR, CD, 640), BF),
            pltpu.VMEM((PLANE * 8, 128), F32),
            pltpu.VMEM((PLANE, 8, 128), BF),
            pltpu.VMEM((PLANE, 8, 128), BF),
            pltpu.VMEM((NLAT, RD, 256), BF),
            pltpu.VMEM((PLANE, RD, ND), BF),
            pltpu.VMEM((NLAT, 2, 128), F32),
            pltpu.VMEM((PLANE, 2, 128), F32),
            dma((8,)),
        ]
        + [dma((PLANE,)), dma((PLANE,))] * 2
        + [dma((NVAR,)), dma((NVAR,))]
        + [dma((PLANE,)), dma((PLANE,))] * 3,
        compiler_params=pltpu.CompilerParams(
            collective_id=0, has_side_effects=True, vmem_limit_bytes=32 * 1024 * 1024
        ),
        name="spectral_layer",
    )(state, *(jnp.asarray(t) for t in tabs), weights_in, bias_in, weights_out)
    return field, zonal.reshape(1, CD, RD), energy[0, :CD]


def solution(mesh):
    return jax.shard_map(
        body,
        mesh=mesh,
        in_specs=(P(None, "var", "lat", "lon"), P(), P(), P()),
        out_specs=(P(None, "var", "lat", "lon"), P(None, "var", "lat"), P("var")),
        check_vma=False,
    )
```

time: 135 us -> 77.4 us (0.57)
  waiting for transfers between devices: 67.2 us -> 0 us
  Pallas kernels: 0 us -> 65.8 us
  starting transfers between devices: 41.8 us -> 0 us
  matrix products: 8.46 us -> 0 us
  other arithmetic: 4.04 us -> 0 us
    all_to_all x8 -> x0, waiting for transfers between devices: 67.2 us -> none  [the longest x5 44.3 us: from_everyone(): lax.all_to_all(jnp.broadcast_to(shard[None], (peers, *shard.shape)), axis...]
    pallas_call x0 -> x1, Pallas kernels: none -> 65.8 us  [body(): pl.pallas_call(lambda *refs: kernel(total_area, *refs), out_shape=(jax.Sh...]
    all_to_all x8 -> x0, starting transfers between devices: 41.8 us -> none  [the longest x5 27.2 us: from_everyone(): lax.all_to_all(jnp.broadcast_to(shard[None], (peers, *shard.shape)), axis...]
    dot_general x5 -> x0, matrix products: 8.46 us -> none  [the longest x1 6.56 us: body(): jnp.einsum('pbcnk,pkl->bcnl', gathered_copies(latback, 'lon', 4), table,...]
    unnamed x9 -> x20, local copies, waits for them, and re-layouts: 1.59 us -> 9.98 us
    broadcast_in_dim x6 -> x0, local copies, waits for them, and re-layouts: 3.66 us -> none  [from_everyone(): jnp.broadcast_to(shard[None], (peers, *shard.shape))]
    transpose x4 -> x0, local copies, waits for them, and re-layouts: 1.63 us -> none  [the longest x1 1.22 us: split_up(): return jnp.moveaxis(shard.reshape(*before, peers, -1, *after), dim, 0)]
    neg x3 -> x0, other arithmetic: 1.57 us -> none  [the longest x1 1.55 us: lon_forward(): -jnp.sin(angle)]
  transfers between devices with their start and end apart: 8 -> 0, of which waited for: 8 -> 0; matrix products, arithmetic and copies ran while one was open for 3% -> 0% of each run, Pallas kernels for 0% -> 0%
where the time goes in v1:
time: 77.4 us; the launch traced here: 77 us
  Pallas kernels  65.8 us (85%)
  local copies, waits for them, and re-layouts  10.5 us (14%)
    pallas_call x1, Pallas kernels, body(): pl.pallas_call(lambda *refs: kernel(total_area, *refs), out_shape=(jax.Sh...  65.8 us
    unnamed x20, local copies, waits for them, and re-layouts  9.98 us

profile of v1, /device:TPU:1, one launch (start us, length us, event | category | flops | bytes accessed | tf_op | source)
XLA Modules:
  0.0 77.0 jit_solution(16263087294453940570)
XLA Ops:
  0.6 0.0 copy-start
  0.6 1.1 %copy-done = bf16[1,32,96,128]{3,2,1,0:T(8,128)(2,1)S(1)} copy-done((bf16[1,32,96,128]{3,2,1,0:T(8,128)(2,1)S(1)}, bf16[1,32,96,128]{3,2,1,0:T(8,128)(2,1)}, u32[]{:S(2)}) %copy-start) | copy-done | bytes 786456
  1.8 0.0 copy-start.1
  1.8 1.0 %copy-done.1 = bf16[8,256,128]{2,1,0:T(8,128)(2,1)S(1)} copy-done((bf16[8,256,128]{2,1,0:T(8,128)(2,1)S(1)}, bf16[8,256,128]{2,1,0:T(8,128)(2,1)}, u32[]{:S(2)}) %copy-start.1) | copy-done | bytes 524312
  2.8 0.0 copy-start.2
  2.8 1.0 %copy-done.2 = bf16[1024,256]{1,0:T(8,128)(2,1)S(1)} copy-done((bf16[1024,256]{1,0:T(8,128)(2,1)S(1)}, bf16[1024,256]{1,0:T(8,128)(2,1)}, u32[]{:S(2)}) %copy-start.2) | copy-done | bytes 524312
  3.8 0.0 copy-start.3
  3.9 1.0 %copy-done.3 = bf16[768,256]{1,0:T(8,128)(2,1)S(1)} copy-done((bf16[768,256]{1,0:T(8,128)(2,1)S(1)}, bf16[768,256]{1,0:T(8,128)(2,1)}, u32[]{:S(2)}) %copy-start.3) | copy-done | bytes 393240
  4.8 0.0 copy-start.4
  4.8 1.0 %copy-done.4 = bf16[256,768]{1,0:T(8,128)(2,1)S(1)} copy-done((bf16[256,768]{1,0:T(8,128)(2,1)S(1)}, bf16[256,768]{1,0:T(8,128)(2,1)}, u32[]{:S(2)}) %copy-start.4) | copy-done | bytes 393240
  5.8 0.0 copy-start.5
  5.8 0.9 %copy-done.5 = bf16[2,256,256]{2,1,0:T(8,128)(2,1)S(1)} copy-done((bf16[2,256,256]{2,1,0:T(8,128)(2,1)S(1)}, bf16[2,256,256]{2,1,0:T(8,128)(2,1)}, u32[]{:S(2)}) %copy-start.5) | copy-done | bytes 262168
  6.8 0.0 copy-start.6
  6.8 0.9 %copy-done.6 = bf16[2,256,256]{2,1,0:T(8,128)(2,1)S(1)} copy-done((bf16[2,256,256]{2,1,0:T(8,128)(2,1)S(1)}, bf16[2,256,256]{2,1,0:T(8,128)(2,1)}, u32[]{:S(2)}) %copy-start.6) | copy-done | bytes 262168
  7.7 0.0 copy-start.7
  7.7 0.7 copy-done.7
  8.5 0.0 copy-start.8
  8.5 0.7 copy-done.8
  9.1 65.8 %spectral_layer.1 = (bf16[1,32,96,128]{3,2,1,0:T(8,128)(2,1)S(1)}, f32[32,96]{1,0:T(8,128)S(1)}, f32[1,128]{1,0:T(1,128)S(1)}) custom-call(bf16[1,32,96,128]{3,2,1,0:T(8,128)(2,1)S(1)} %copy-done, bf16[1024,256]{1,0:T(8,128)(2,1)S(1)} %copy-done.2, bf16[256,768]{1,0:T(8,128)(2,1)S(1)} %copy-done.4, bf16[768,256]{1,0:T(8,128)(2,1)S(1)} %copy-done.3, ...), custom_call_target="tpu_custom_call" | custom-call | tf_op jit(solution)/shard_map/spectral_layer/pallas_call | solution.py:457
  75.0 0.5 slice_bitcast_fusion
  75.5 0.9 %copy.14 = bf16[1,32,96,128]{3,2,1,0:T(8,128)(2,1)} copy(bf16[1,32,96,128]{3,2,1,0:T(8,128)(2,1)S(1)} %get-tuple-element.12) | data formatting | bytes 1572864
  76.4 0.6 copy.15
Async XLA Ops:
  0.6 1.1 %copy-start = (bf16[1,32,96,128]{3,2,1,0:T(8,128)(2,1)S(1)}, bf16[1,32,96,128]{3,2,1,0:T(8,128)(2,1)}, u32[]{:S(2)}) copy-start(bf16[1,32,96,128]{3,2,1,0:T(8,128)(2,1)} %refs_0_.1) | copy-start | bytes 2359300
  1.8 1.0 %copy-start.1 = (bf16[8,256,128]{2,1,0:T(8,128)(2,1)S(1)}, bf16[8,256,128]{2,1,0:T(8,128)(2,1)}, u32[]{:S(2)}) copy-start(bf16[8,256,128]{2,1,0:T(8,128)(2,1)} %constant.13.clone.refs_4_) | copy-start | bytes 1572868
  2.8 1.0 %copy-start.2 = (bf16[1024,256]{1,0:T(8,128)(2,1)S(1)}, bf16[1024,256]{1,0:T(8,128)(2,1)}, u32[]{:S(2)}) copy-start(bf16[1024,256]{1,0:T(8,128)(2,1)} %constant.10.clone.refs_1_) | copy-start | bytes 1572868
  3.8 1.0 %copy-start.3 = (bf16[768,256]{1,0:T(8,128)(2,1)S(1)}, bf16[768,256]{1,0:T(8,128)(2,1)}, u32[]{:S(2)}) copy-start(bf16[768,256]{1,0:T(8,128)(2,1)} %constant.12.clone.refs_3_) | copy-start | bytes 1179652
  4.8 1.0 %copy-start.4 = (bf16[256,768]{1,0:T(8,128)(2,1)S(1)}, bf16[256,768]{1,0:T(8,128)(2,1)}, u32[]{:S(2)}) copy-start(bf16[256,768]{1,0:T(8,128)(2,1)} %constant.11.clone.refs_2_) | copy-start | bytes 1179652
  5.8 0.9 %copy-start.5 = (bf16[2,256,256]{2,1,0:T(8,128)(2,1)S(1)}, bf16[2,256,256]{2,1,0:T(8,128)(2,1)}, u32[]{:S(2)}) copy-start(bf16[2,256,256]{2,1,0:T(8,128)(2,1)} %refs_6_.1) | copy-start | bytes 786436
  6.8 0.9 %copy-start.6 = (bf16[2,256,256]{2,1,0:T(8,128)(2,1)S(1)}, bf16[2,256,256]{2,1,0:T(8,128)(2,1)}, u32[]{:S(2)}) copy-start(bf16[2,256,256]{2,1,0:T(8,128)(2,1)} %refs_8_.1) | copy-start | bytes 786436
  7.7 0.7 copy-start.7
  8.5 0.7 copy-start.8

commit v2 on v1

v2 whole, which is shorter than its diff:
```python
import math

import jax
import jax.numpy as jnp
import numpy as np
from jax import lax
from jax.experimental import pallas as pl
from jax.experimental.pallas import tpu as pltpu
from jax.sharding import PartitionSpec as P

LAT = 384
LON = 1024
MLAT = 96
MLON = 96
NVAR = 8
NLAT = 4
NLON = 8
PLANE = NLAT * NLON
CD = 32
RD = LAT // NLAT
ND = LON // NLON
JO = MLAT // PLANE
MESH = pl.DeviceIdType.MESH
TAIL_AT = 0.23
TAIL = (
    0.09190782232377631,
    0.08914107185889676,
    0.10610870974692016,
    -0.0007481814870291388,
    0.25362340835459335,
    -0.23501017104744312,
    0.2688627946887361,
    -0.0738853870258165,
)
BF = jnp.bfloat16
F32 = jnp.float32


def ring(d):
    return min(d, 4 - d)


CHIPS = sorted(((i, j) for i in range(4) for j in range(4) if i or j), key=lambda c: -ring(c[0]) - ring(c[1]))
PEERS = [(i, j, c) for i, j in CHIPS for c in range(2)] + [(0, 0, 1)]


def gelu(x):
    size = jnp.abs(x)
    t = 1.0 / (1.0 + TAIL_AT * size)
    poly = TAIL[-1]
    for c in TAIL[-2::-1]:
        poly = poly * t + c
    tail = (size * t) * poly * jnp.exp2((x * x) * (-0.5 / math.log(2.0)))
    return jnp.maximum(x, 0.0) - tail


def tables():
    k = np.arange(MLON)
    n = np.arange(LON)
    angle = 2.0 * np.pi / LON * ((n[:, None] * k[None, :]) % LON)
    scale = 1.0 / math.sqrt(LAT * LON)
    etab = np.zeros((LON, 256), np.float32)
    etab[:, :MLON] = np.cos(angle) * scale
    etab[:, 128 : 128 + MLON] = -np.sin(angle) * scale
    weight = np.where(k == 0, 1.0, 2.0)[:, None] * scale
    full = np.zeros((256, LON), np.float32)
    full[:MLON] = weight * np.cos(angle.T)
    full[128 : 128 + MLON] = -weight * np.sin(angle.T)
    htab = full.reshape(256, 4, 2 * ND).transpose(1, 0, 2)
    r = np.arange(LAT)
    freqs = np.arange(MLAT) - MLAT // 2
    turn = 2.0 * np.pi / LAT * np.mod(freqs[:, None] * r[None, :], LAT)
    cosine, sine = np.cos(turn), np.sin(turn)
    forward = np.zeros((PLANE, 8, 2, LAT), np.float32)
    forward[:, 0:3, 0] = cosine.reshape(PLANE, JO, LAT)
    forward[:, 0:3, 1] = sine.reshape(PLANE, JO, LAT)
    forward[:, 3:6, 0] = -sine.reshape(PLANE, JO, LAT)
    forward[:, 3:6, 1] = cosine.reshape(PLANE, JO, LAT)
    qtab = forward.reshape(PLANE * 8, 2 * LAT)
    rtab = qtab.T
    area = np.cos(np.pi * ((r + 0.5) / LAT - 0.5))
    gtab = np.broadcast_to(area.reshape(NLAT, 1, RD), (NLAT, 8, RD))
    bf = lambda t: np.ascontiguousarray(t).astype(jnp.bfloat16)
    return (
        bf(etab),
        bf(qtab),
        bf(rtab),
        bf(htab),
        np.ascontiguousarray(gtab).astype(np.float32),
        float(LON * area.sum()),
    )


SCOPES = []


def scope(name):
    while SCOPES:
        SCOPES.pop().__exit__(None, None, None)
    if name:
        SCOPES.append(jax.named_scope(name))
        SCOPES[-1].__enter__()


def kernel(
    total_area,
    state,
    etab,
    qtab,
    rtab,
    htab,
    gtab,
    win,
    bias,
    wout,
    field,
    stats,
    st,
    ev,
    qv,
    rv,
    hv,
    gv,
    wiv,
    wov,
    bcol,
    xin,
    lv,
    sbuf,
    srecv,
    xf,
    xall,
    mf,
    mbuf,
    mrecv,
    lbv,
    fs,
    acc,
    acc2,
    zst,
    load_sem,
    s1,
    r1,
    s2,
    r2,
    s3,
    r3,
    s4,
    r4,
    s5,
    r5,
    s6,
    r6,
):
    v = lax.axis_index("var")
    a = lax.axis_index("lat")
    b = lax.axis_index("lon")
    y, core = lax.div(b, 2), lax.rem(b, 2)

    def slot_of(pa, py, pc):
        return pc * 16 + pa * 4 + py

    me = slot_of(a, y, core)
    lats = [lax.rem(a + i, 4) for i in range(4)]
    ys = [lax.rem(y + i, 4) for i in range(4)]
    cores = [core, 1 - core]

    def plane(peer):
        i, j, c = peer
        pa, py, pc = lats[i], ys[j], cores[c]
        return {"lat": pa, "lon": py * 2 + pc}, slot_of(pa, py, pc)

    def at_slot(slot):
        pa, py, pc = lax.div(lax.rem(slot, 16), 4), lax.rem(slot, 4), lax.div(slot, 16)
        return {"lat": pa, "lon": py * 2 + pc}

    scope("greet")
    barrier = pltpu.get_barrier_semaphore()
    for peer in PEERS:
        pl.semaphore_signal(barrier, inc=1, device_id=plane(peer)[0], device_id_type=MESH)
    far = (4, 3, 5, 2, 6, 1, 7)
    vars_ = {d: lax.rem(v + d, NVAR) for d in far}
    for d in far:
        pl.semaphore_signal(barrier, inc=1, device_id={"var": vars_[d]}, device_id_type=MESH)

    loads = [
        pltpu.make_async_copy(src, dst, load_sem.at[i])
        for i, (src, dst) in enumerate(
            [
                (state.at[0], st),
                (bias, bcol.at[0:2]),
                (etab, ev),
                (qtab, qv),
                (win, wiv),
                (wout, wov),
                (rtab, rv),
                (htab, hv),
                (gtab, gv),
            ]
        )
    ]
    for load in loads:
        load.start()
    mf[...] = jnp.zeros_like(mf)
    zst[...] = jnp.zeros_like(zst)
    acc[...] = jnp.zeros_like(acc)
    acc2[...] = jnp.zeros_like(acc2)
    scope("barrier")
    loads[0].wait()
    pl.semaphore_wait(barrier, PLANE - 1 + NVAR - 1)

    def all_but_me(first, last, wait):
        def step(slot, _):
            @pl.when(slot != me)
            def _():
                wait(slot)

            return 0

        lax.fori_loop(first, last, step, 0)

    def copy1(src, dst, to):
        return pltpu.make_async_remote_copy(
            src_ref=st.at[src],
            dst_ref=xin.at[dst],
            send_sem=s1.at[src],
            recv_sem=r1.at[dst],
            device_id=to,
            device_id_type=MESH,
        )

    scope("send1")
    for pc in range(2):
        for i, j in [*CHIPS, (0, 0)]:
            slot = slot_of(lats[i], ys[j], pc)

            def start(i=i, j=j, slot=slot):
                copy1(slot, me, {"lat": lats[i], "lon": ys[j] * 2 + pc}).start()

            if i or j:
                start()
            else:
                pl.when(core != pc)(start)
    xin[me] = st[me]
    scope("wait1")
    loads[1].wait()
    turned = jnp.transpose(bcol[...])
    bias_r = jnp.broadcast_to(turned[:, 0:1], (256, 128))
    bias_i = jnp.broadcast_to(turned[:, 1:2], (256, 128))
    loads[2].wait()
    for da in (0, 1, 3, 2):
        pa = lats[da]

        def wait1(i, _):
            slot = lax.div(i, 4) * 16 + pa * 4 + lax.rem(i, 4)

            @pl.when(slot != me)
            def _():
                copy1(slot, slot, at_slot(slot)).wait_recv()

            return 0

        lax.fori_loop(0, NLON, wait1, 0)
        rows = jnp.concatenate([xin[(i % 2) * 16 + pa * 4 + i // 2] for i in range(NLON)], axis=1)
        lv[pa] = jnp.dot(rows, ev[...], preferred_element_type=F32).astype(BF)

    scope("fwd")
    loads[3].wait()
    lon = lv[...].reshape(LAT, 256)
    spec = jnp.dot(qv[:, 0:LAT], lon[:, 0:128], preferred_element_type=F32)
    spec += jnp.dot(qv[:, LAT : 2 * LAT], lon[:, 128:256], preferred_element_type=F32)
    sbuf[...] = spec.reshape(PLANE, 8, 128).astype(BF)

    def copy2(src, dst, to):
        return pltpu.make_async_remote_copy(
            src_ref=sbuf.at[src],
            dst_ref=srecv.at[dst],
            send_sem=s2.at[src],
            recv_sem=r2.at[dst],
            device_id=to,
            device_id_type=MESH,
        )

    scope("send2")
    for peer in PEERS:
        to, slot = plane(peer)
        copy2(slot, me, to).start()
    srecv[me] = sbuf[me]

    lane = lax.broadcasted_iota(jnp.int32, (16, 128), 1)
    low, high = lane < 32, lane >= 96
    second = jnp.logical_and(lane >= 32, lane < 64)

    def packed(t0, t1, t2):
        up, half = pltpu.roll(t2, 96, 1), pltpu.roll(t2, 64, 1)
        return jnp.where(high, up, t0), jnp.where(high, half, t1), up, half

    def copy3(half, d, slot):
        part = xall.at[slot, pl.ds(half * 16, 16)]
        return pltpu.make_async_remote_copy(
            src_ref=part,
            dst_ref=part,
            send_sem=s3.at[half, d],
            recv_sem=r3.at[half, slot],
            device_id={"var": vars_[d]},
            device_id_type=MESH,
        )

    for half in range(2):
        scope(f"wait2_{half}")
        all_but_me(half * 16, half * 16 + 16, lambda slot: copy2(slot, slot, at_slot(slot)).wait_recv())
        scope(f"pack_{half}")
        xf[...] = srecv[half * 16 : half * 16 + 16].astype(F32).reshape(128, 128)
        t = [xf[pl.ds(i, 16, stride=8), :] for i in range(6)]
        p0, p1, _, last_r = packed(*t[0:3])
        p2, p3, last_i, _ = packed(*t[3:6])
        p4 = jnp.where(low, last_r, jnp.where(second, last_i, 0.0))
        xall[v, half * 16 : half * 16 + 16] = jnp.concatenate([p0, p1, p2, p3, p4], axis=1).astype(BF)
        for d in far:
            copy3(half, d, v).start()

    scope("wait3")
    loads[4].wait()
    loads[5].wait()
    for half in range(2):
        for d in reversed(far):
            copy3(half, d, vars_[d]).wait_recv()
    scope("mix")
    every = xall[...].reshape(NVAR * CD, 640)

    def combined(g, half):
        re = g[:half, 0:256] - g[half:, 256:512]
        im = g[half:, 0:256] + g[:half, 256:512]
        gr, gi = g[:half, 512:640], g[half:, 512:640]
        which = lax.broadcasted_iota(jnp.int32, (half, 128), 1) < 32
        last = jnp.where(which, gr - pltpu.roll(gi, 96, 1), gr + pltpu.roll(gi, 32, 1))
        return re, im, last, which

    g = jnp.dot(wiv[...].reshape(512, 256), every, preferred_element_type=F32)
    re, im, last, which = combined(g, 256)
    wide_r = jnp.concatenate([bias_r, bias_r], axis=1)
    wide_i = jnp.concatenate([bias_i, bias_i], axis=1)
    hidden = jnp.concatenate(
        [re + wide_r, im + wide_i, last + jnp.where(which, bias_r, bias_i)], axis=1
    )
    hidden = jnp.maximum(hidden, 0.0).astype(BF)
    first = pl.multiple_of(v * CD, CD)
    own = jnp.concatenate([wov[0, pl.ds(first, CD), :], wov[1, pl.ds(first, CD), :]], axis=0)
    g = jnp.dot(own, hidden, preferred_element_type=F32)
    re, im, last, _ = combined(g, CD)
    lane = lax.broadcasted_iota(jnp.int32, (CD, 128), 1)
    sel = [lane < 32, lane < 64]
    t2 = jnp.where(
        sel[0],
        pltpu.roll(re[:, 0:128], 32, 1),
        jnp.where(sel[1], pltpu.roll(re[:, 128:256], 64, 1), pltpu.roll(last, 64, 1)),
    )
    t5 = jnp.where(
        sel[0],
        pltpu.roll(im[:, 0:128], 32, 1),
        jnp.where(sel[1], pltpu.roll(im[:, 128:256], 64, 1), pltpu.roll(last, 32, 1)),
    )
    for i, tile in enumerate([re[:, 0:128], re[:, 128:256], t2, im[:, 0:128], im[:, 128:256], t5]):
        mf[pl.ds(i, PLANE, stride=8), :] = tile
    mbuf[...] = mf[...].reshape(PLANE, 8, 128).astype(BF)

    def copy4(src, dst, to):
        return pltpu.make_async_remote_copy(
            src_ref=mbuf.at[src],
            dst_ref=mrecv.at[dst],
            send_sem=s4.at[src],
            recv_sem=r4.at[dst],
            device_id=to,
            device_id_type=MESH,
        )

    scope("send4")
    for peer in PEERS:
        to, slot = plane(peer)
        copy4(slot, me, to).start()
    mrecv[me] = mbuf[me]
    scope("wait4")
    for load in loads[6:]:
        load.wait()
    all_but_me(0, PLANE, lambda slot: copy4(slot, slot, at_slot(slot)).wait_recv())
    scope("back")
    modes = mrecv[...].reshape(PLANE * 8, 128)
    back_r = jnp.dot(rv[0:LAT, :], modes, preferred_element_type=F32)
    back_i = jnp.dot(rv[LAT : 2 * LAT, :], modes, preferred_element_type=F32)
    lbv[...] = jnp.concatenate([back_r, back_i], axis=1).astype(BF).reshape(NLAT, RD, 256)

    def copy5(src, dst, to):
        return pltpu.make_async_remote_copy(
            src_ref=fs.at[src],
            dst_ref=field.at[0, dst],
            send_sem=s5.at[src],
            recv_sem=r5.at[dst],
            device_id=to,
            device_id_type=MESH,
        )

    def chip(i, j):
        pa, py = lats[i], ys[j]
        act = gelu(jnp.dot(lbv[pa], hv[py], preferred_element_type=F32))
        fs[slot_of(pa, py, 0)] = act[:, 0:128].astype(BF)
        fs[slot_of(pa, py, 1)] = act[:, 128:256].astype(BF)
        acc[pa] += act[:, 0:128] + act[:, 128:256]
        square = act * act
        acc2[pa] += square[:, 0:128] + square[:, 128:256]

    def send5(peer):
        to, slot = plane(peer)
        copy5(slot, me, to).start()

    scope("gelu")
    near = [c for c in CHIPS if ring(c[0]) + ring(c[1]) == 1]
    for c in CHIPS:
        chip(*c)
        if c not in near:
            send5((*c, 0))
            send5((*c, 1))
    chip(0, 0)
    scope("stats")
    ones = jnp.ones((8, 128), F32)
    weighted = jnp.zeros((8, 128), F32)
    for band in range(NLAT):
        rowsum = lax.dot_general(
            ones,
            acc[band],
            (((1,), (1,)), ((), ())),
            precision=lax.Precision.HIGHEST,
            preferred_element_type=F32,
        )
        zst[band, 0:1, 0:RD] = rowsum[0:1] * (1.0 / LON)
        weighted += jnp.dot(
            gv[band], acc2[band], precision=lax.Precision.HIGHEST, preferred_element_type=F32
        )
    total = jnp.sum(weighted, axis=1, keepdims=True)[0:1] * (1.0 / total_area)
    mine = jnp.where(lax.broadcasted_iota(jnp.int32, (1, 128), 1) == me, total, 0.0)
    for band in range(NLAT):
        zst[band, 1:2, :] = mine

    def copy6(src, dst, band, to):
        return pltpu.make_async_remote_copy(
            src_ref=zst.at[band],
            dst_ref=stats.at[dst],
            send_sem=s6.at[src],
            recv_sem=r6.at[dst],
            device_id=to,
            device_id_type=MESH,
        )

    scope("send6")
    for peer in PEERS:
        to, slot = plane(peer)
        copy6(slot, me, lats[peer[0]], to).start()
    for c in near:
        send5((*c, 0))
        send5((*c, 1))
    send5((0, 0, 1))
    field[0, me] = fs[me]
    stats[me] = zst[a]
    scope("wait5")

    def ended(slot):
        to = at_slot(slot)
        copy1(slot, slot, to).wait_send()
        copy2(slot, slot, to).wait_send()
        copy4(slot, slot, to).wait_send()

    all_but_me(0, PLANE, ended)
    for half in range(2):
        for d in far:
            copy3(half, d, v).wait_send()

    def arrived(slot):
        to = at_slot(slot)
        copy5(slot, slot, to).wait_send()
        copy6(slot, slot, a, to).wait_send()
        copy5(slot, slot, to).wait_recv()
        copy6(slot, slot, a, to).wait_recv()

    all_but_me(0, PLANE, arrived)
    scope(None)


def finish(field, stats, out, zonal, energy, zv, evec, sems):
    big = pltpu.make_async_copy(field, out, sems.at[0])
    big.start()
    gathered = jnp.zeros((1, 128), F32)
    for i in range(CD):
        both = stats[i]
        zv[0, i : i + 1, :] = both[0:1, 0:RD]
        gathered += both[1:2, :]
    evec[...] = gathered[0, 0:CD]
    small = pltpu.make_async_copy(zv, zonal, sems.at[1])
    small.start()
    other = pltpu.make_async_copy(evec, energy, sems.at[2])
    other.start()
    big.wait()
    small.wait()
    other.wait()


def body(state, weights_in, bias_in, weights_out):
    *tabs, total_area = tables()
    hbm = pl.BlockSpec(memory_space=pltpu.HBM)
    vmem = pl.BlockSpec(memory_space=pltpu.VMEM)
    dma = pltpu.SemaphoreType.DMA
    operands = (state, *(jnp.asarray(t) for t in tabs), weights_in, bias_in, weights_out)
    field, stats = pl.pallas_call(
        lambda *refs: kernel(total_area, *refs),
        out_shape=(
            jax.ShapeDtypeStruct((1, CD, RD, ND), BF),
            jax.ShapeDtypeStruct((PLANE, 2, 128), F32),
        ),
        in_specs=[hbm] * 9,
        out_specs=(vmem, vmem),
        scratch_shapes=[
            pltpu.VMEM((CD, RD, ND), BF),
            pltpu.VMEM((LON, 256), BF),
            pltpu.VMEM((256, 2 * LAT), BF),
            pltpu.VMEM((2 * LAT, 256), BF),
            pltpu.VMEM((4, 256, 256), BF),
            pltpu.VMEM((NLAT, 8, RD), F32),
            pltpu.VMEM((2, 256, 256), BF),
            pltpu.VMEM((2, 256, 256), BF),
            pltpu.VMEM((128, 256), F32),
            pltpu.VMEM((PLANE, RD, ND), BF),
            pltpu.VMEM((NLAT, RD, 256), BF),
            pltpu.VMEM((PLANE, 8, 128), BF),
            pltpu.VMEM((PLANE, 8, 128), BF),
            pltpu.VMEM((128, 128), F32),
            pltpu.VMEM((NVAR, CD, 640), BF),
            pltpu.VMEM((PLANE * 8, 128), F32),
            pltpu.VMEM((PLANE, 8, 128), BF),
            pltpu.VMEM((PLANE, 8, 128), BF),
            pltpu.VMEM((NLAT, RD, 256), BF),
            pltpu.VMEM((PLANE, RD, ND), BF),
            pltpu.VMEM((NLAT, RD, 128), F32),
            pltpu.VMEM((NLAT, RD, 128), F32),
            pltpu.VMEM((NLAT, 2, 128), F32),
            dma((9,)),
        ]
        + [dma((PLANE,)), dma((PLANE,))] * 2
        + [dma((2, NVAR)), dma((2, NVAR))]
        + [dma((PLANE,)), dma((PLANE,))] * 3,
        compiler_params=pltpu.CompilerParams(
            collective_id=0, has_side_effects=True, vmem_limit_bytes=32 * 1024 * 1024
        ),
        name="spectral_layer",
    )(*(pltpu.with_memory_space_constraint(x, pltpu.HBM) for x in operands))
    return pl.pallas_call(
        finish,
        out_shape=(
            jax.ShapeDtypeStruct((1, CD, RD, ND), BF),
            jax.ShapeDtypeStruct((1, CD, RD), F32),
            jax.ShapeDtypeStruct((CD,), F32),
        ),
        in_specs=[vmem, vmem],
        out_specs=(hbm, hbm, hbm),
        scratch_shapes=[
            pltpu.VMEM((1, CD, RD), F32),
            pltpu.VMEM((CD,), F32),
            dma((3,)),
        ],
        compiler_params=pltpu.CompilerParams(vmem_limit_bytes=8 * 1024 * 1024),
        name="finish",
    )(field, stats)


def solution(mesh):
    return jax.shard_map(
        body,
        mesh=mesh,
        in_specs=(P(None, "var", "lat", "lon"), P(), P(), P()),
        out_specs=(P(None, "var", "lat", "lon"), P(None, "var", "lat"), P("var")),
        check_vma=False,
    )
```

time: 77.4 us -> 60 us (0.78)
  local copies, waits for them, and re-layouts: 10.5 us -> 0 us
  Pallas kernels: 65.8 us -> 59.2 us
    unnamed x20 -> x0, local copies, waits for them, and re-layouts: 9.98 us -> none
    pallas_call x1, Pallas kernels: 65.8 us -> 58.3 us  [body(): pl.pallas_call(lambda *refs: kernel(total_area, *refs), out_shape=(jax.Sh...]
    pallas_call x0 -> x1, Pallas kernels: none -> 0.91 us  [body(): pl.pallas_call(finish, out_shape=(jax.ShapeDtypeStruct((1, CD, RD, ND), B...]
where the time goes in v2:
time: 60 us; the launch traced here: 59.9 us
  Pallas kernels  59.2 us (99%)
  between operations  0.64 us (1%)
    pallas_call x1, Pallas kernels, body(): pl.pallas_call(lambda *refs: kernel(total_area, *refs), out_shape=(jax.Sh...  58.3 us

profile of v2, /device:TPU:1, one launch (start us, length us, event | category | flops | bytes accessed | tf_op | source)
XLA Modules:
  0.0 59.9 jit_solution(1134631492066273649)
XLA Ops:
  0.6 58.3 %spectral_layer.1 = (bf16[1,32,96,128]{3,2,1,0:T(8,128)(2,1)S(1)}, f32[32,2,128]{2,1,0:T(2,128)S(1)}) custom-call(bf16[1,32,96,128]{3,2,1,0:T(8,128)(2,1)} %refs_0_.1, bf16[1024,256]{1,0:T(8,128)(2,1)} %constant.10.clone.refs_1_, bf16[256,768]{1,0:T(8,128)(2,1)} %constant.11.clone.refs_2_, bf16[768,256]{1,0:T(8,128)(2,1)} %constant.12.clone.refs_3_, ...), custom_call_target="tpu_custom_call" | custom-call | tf_op jit(solution)/shard_map/spectral_layer/pallas_call | solution.py:511
  59.0 0.9 %finish.1 = (bf16[1,32,96,128]{3,2,1,0:T(8,128)(2,1)}, f32[1,32,96]{2,1,0:T(8,128)}, f32[32]{0:T(128)}) custom-call(bf16[1,32,96,128]{3,2,1,0:T(8,128)(2,1)S(1)} %get-tuple-element.5.field, f32[32,2,128]{2,1,0:T(2,128)S(1)} %get-tuple-element.6.stats), custom_call_target="tpu_custom_call" | custom-call | tf_op jit(solution)/shard_map/finish/pallas_call | solution.py:553

commit v3 on v2

--- a/solution.py
+++ b/solution.py
@@ -170,19 +170,6 @@
         pa, py, pc = lats[i], ys[j], cores[c]
         return {"lat": pa, "lon": py * 2 + pc}, slot_of(pa, py, pc)
 
-    def at_slot(slot):
-        pa, py, pc = lax.div(lax.rem(slot, 16), 4), lax.rem(slot, 4), lax.div(slot, 16)
-        return {"lat": pa, "lon": py * 2 + pc}
-
-    scope("greet")
-    barrier = pltpu.get_barrier_semaphore()
-    for peer in PEERS:
-        pl.semaphore_signal(barrier, inc=1, device_id=plane(peer)[0], device_id_type=MESH)
-    far = (4, 3, 5, 2, 6, 1, 7)
-    vars_ = {d: lax.rem(v + d, NVAR) for d in far}
-    for d in far:
-        pl.semaphore_signal(barrier, inc=1, device_id={"var": vars_[d]}, device_id_type=MESH)
-
     loads = [
         pltpu.make_async_copy(src, dst, load_sem.at[i])
         for i, (src, dst) in enumerate(
@@ -199,7 +186,17 @@
             ]
         )
     ]
-    for load in loads:
+    loads[0].start()
+    scope("greet")
+    barrier = pltpu.get_barrier_semaphore()
+    for peer in PEERS:
+        pl.semaphore_signal(barrier, inc=1, device_id=plane(peer)[0], device_id_type=MESH)
+    far = (4, 3, 5, 2, 6, 1, 7)
+    vars_ = {d: lax.rem(v + d, NVAR) for d in far}
+    for d in far:
+        pl.semaphore_signal(barrier, inc=1, device_id={"var": vars_[d]}, device_id_type=MESH)
+
+    for load in loads[1:]:
         load.start()
     mf[...] = jnp.zeros_like(mf)
     zst[...] = jnp.zeros_like(zst)
@@ -209,38 +206,24 @@
     loads[0].wait()
     pl.semaphore_wait(barrier, PLANE - 1 + NVAR - 1)
 
-    def all_but_me(first, last, wait):
-        def step(slot, _):
-            @pl.when(slot != me)
-            def _():
-                wait(slot)
-
-            return 0
-
-        lax.fori_loop(first, last, step, 0)
-
-    def copy1(src, dst, to):
+    def whole(ref, sem):
+        some = ref.at[pl.ds(0, PLANE - 1)]
+        pltpu.make_async_copy(some, some, sem.at[0]).wait()
+
+    def copy1(src, dst, band, to):
         return pltpu.make_async_remote_copy(
             src_ref=st.at[src],
             dst_ref=xin.at[dst],
-            send_sem=s1.at[src],
-            recv_sem=r1.at[dst],
+            send_sem=s1.at[0],
+            recv_sem=r1.at[band],
             device_id=to,
             device_id_type=MESH,
         )
 
     scope("send1")
-    for pc in range(2):
-        for i, j in [*CHIPS, (0, 0)]:
-            slot = slot_of(lats[i], ys[j], pc)
-
-            def start(i=i, j=j, slot=slot):
-                copy1(slot, me, {"lat": lats[i], "lon": ys[j] * 2 + pc}).start()
-
-            if i or j:
-                start()
-            else:
-                pl.when(core != pc)(start)
+    for peer in PEERS:
+        to, slot = plane(peer)
+        copy1(slot, me, a, to).start()
     xin[me] = st[me]
     scope("wait1")
     loads[1].wait()
@@ -251,16 +234,8 @@
     for da in (0, 1, 3, 2):
         pa = lats[da]
 
-        def wait1(i, _):
-            slot = lax.div(i, 4) * 16 + pa * 4 + lax.rem(i, 4)
-
-            @pl.when(slot != me)
-            def _():
-                copy1(slot, slot, at_slot(slot)).wait_recv()
-
-            return 0
-
-        lax.fori_loop(0, NLON, wait1, 0)
+        some = xin.at[pl.ds(0, NLON if da else NLON - 1)]
+        pltpu.make_async_copy(some, some, r1.at[pa]).wait()
         rows = jnp.concatenate([xin[(i % 2) * 16 + pa * 4 + i // 2] for i in range(NLON)], axis=1)
         lv[pa] = jnp.dot(rows, ev[...], preferred_element_type=F32).astype(BF)
 
@@ -275,8 +250,8 @@
         return pltpu.make_async_remote_copy(
             src_ref=sbuf.at[src],
             dst_ref=srecv.at[dst],
-            send_sem=s2.at[src],
-            recv_sem=r2.at[dst],
+            send_sem=s2.at[0],
+            recv_sem=r2.at[0],
             device_id=to,
             device_id_type=MESH,
         )
@@ -287,7 +262,12 @@
         copy2(slot, me, to).start()
     srecv[me] = sbuf[me]
 
-    lane = lax.broadcasted_iota(jnp.int32, (16, 128), 1)
+    scope("wait2")
+    whole(srecv, r2)
+    scope("pack")
+    xf[...] = srecv[...].astype(F32).reshape(PLANE * 8, 128)
+    t = [xf[pl.ds(i, PLANE, stride=8), :] for i in range(6)]
+    lane = lax.broadcasted_iota(jnp.int32, (PLANE, 128), 1)
     low, high = lane < 32, lane >= 96
     second = jnp.logical_and(lane >= 32, lane < 64)
 
@@ -295,36 +275,25 @@
         up, half = pltpu.roll(t2, 96, 1), pltpu.roll(t2, 64, 1)
         return jnp.where(high, up, t0), jnp.where(high, half, t1), up, half
 
-    def copy3(half, d, slot):
-        part = xall.at[slot, pl.ds(half * 16, 16)]
-        return pltpu.make_async_remote_copy(
-            src_ref=part,
-            dst_ref=part,
-            send_sem=s3.at[half, d],
-            recv_sem=r3.at[half, slot],
+    p0, p1, _, last_r = packed(*t[0:3])
+    p2, p3, last_i, _ = packed(*t[3:6])
+    p4 = jnp.where(low, last_r, jnp.where(second, last_i, 0.0))
+    xall[v] = jnp.concatenate([p0, p1, p2, p3, p4], axis=1).astype(BF)
+    for d in far:
+        pltpu.make_async_remote_copy(
+            src_ref=xall.at[v],
+            dst_ref=xall.at[v],
+            send_sem=s3.at[0],
+            recv_sem=r3.at[0],
             device_id={"var": vars_[d]},
             device_id_type=MESH,
-        )
-
-    for half in range(2):
-        scope(f"wait2_{half}")
-        all_but_me(half * 16, half * 16 + 16, lambda slot: copy2(slot, slot, at_slot(slot)).wait_recv())
-        scope(f"pack_{half}")
-        xf[...] = srecv[half * 16 : half * 16 + 16].astype(F32).reshape(128, 128)
-        t = [xf[pl.ds(i, 16, stride=8), :] for i in range(6)]
-        p0, p1, _, last_r = packed(*t[0:3])
-        p2, p3, last_i, _ = packed(*t[3:6])
-        p4 = jnp.where(low, last_r, jnp.where(second, last_i, 0.0))
-        xall[v, half * 16 : half * 16 + 16] = jnp.concatenate([p0, p1, p2, p3, p4], axis=1).astype(BF)
-        for d in far:
-            copy3(half, d, v).start()
+        ).start()
 
     scope("wait3")
     loads[4].wait()
     loads[5].wait()
-    for half in range(2):
-        for d in reversed(far):
-            copy3(half, d, vars_[d]).wait_recv()
+    others = xall.at[pl.ds(0, NVAR - 1)]
+    pltpu.make_async_copy(others, others, r3.at[0]).wait()
     scope("mix")
     every = xall[...].reshape(NVAR * CD, 640)
 
@@ -368,8 +337,8 @@
         return pltpu.make_async_remote_copy(
             src_ref=mbuf.at[src],
             dst_ref=mrecv.at[dst],
-            send_sem=s4.at[src],
-            recv_sem=r4.at[dst],
+            send_sem=s4.at[0],
+            recv_sem=r4.at[0],
             device_id=to,
             device_id_type=MESH,
         )
@@ -382,7 +351,7 @@
     scope("wait4")
     for load in loads[6:]:
         load.wait()
-    all_but_me(0, PLANE, lambda slot: copy4(slot, slot, at_slot(slot)).wait_recv())
+    whole(mrecv, r4)
     scope("back")
     modes = mrecv[...].reshape(PLANE * 8, 128)
     back_r = jnp.dot(rv[0:LAT, :], modes, preferred_element_type=F32)
@@ -393,8 +362,8 @@
         return pltpu.make_async_remote_copy(
             src_ref=fs.at[src],
             dst_ref=field.at[0, dst],
-            send_sem=s5.at[src],
-            recv_sem=r5.at[dst],
+            send_sem=s5.at[0],
+            recv_sem=r5.at[0],
             device_id=to,
             device_id_type=MESH,
         )
@@ -413,7 +382,7 @@
         copy5(slot, me, to).start()
 
     scope("gelu")
-    near = [c for c in CHIPS if ring(c[0]) + ring(c[1]) == 1]
+    near = [c for c in CHIPS if ring(c[0]) + ring(c[1]) <= 2]
     for c in CHIPS:
         chip(*c)
         if c not in near:
@@ -444,8 +413,8 @@
         return pltpu.make_async_remote_copy(
             src_ref=zst.at[band],
             dst_ref=stats.at[dst],
-            send_sem=s6.at[src],
-            recv_sem=r6.at[dst],
+            send_sem=s6.at[0],
+            recv_sem=r6.at[0],
             device_id=to,
             device_id_type=MESH,
         )
@@ -462,25 +431,14 @@
     stats[me] = zst[a]
     scope("wait5")
 
-    def ended(slot):
-        to = at_slot(slot)
-        copy1(slot, slot, to).wait_send()
-        copy2(slot, slot, to).wait_send()
-        copy4(slot, slot, to).wait_send()
-
-    all_but_me(0, PLANE, ended)
-    for half in range(2):
-        for d in far:
-            copy3(half, d, v).wait_send()
-
-    def arrived(slot):
-        to = at_slot(slot)
-        copy5(slot, slot, to).wait_send()
-        copy6(slot, slot, a, to).wait_send()
-        copy5(slot, slot, to).wait_recv()
-        copy6(slot, slot, a, to).wait_recv()
-
-    all_but_me(0, PLANE, arrived)
+    whole(st, s1)
+    whole(sbuf, s2)
+    pltpu.make_async_copy(others, others, s3.at[0]).wait()
+    whole(mbuf, s4)
+    whole(fs, s5)
+    whole(stats, s6)
+    whole(field.at[0], r5)
+    whole(stats, r6)
     scope(None)
 
 
@@ -530,7 +488,7 @@
             pltpu.VMEM((NLAT, RD, 256), BF),
             pltpu.VMEM((PLANE, 8, 128), BF),
             pltpu.VMEM((PLANE, 8, 128), BF),
-            pltpu.VMEM((128, 128), F32),
+            pltpu.VMEM((PLANE * 8, 128), F32),
             pltpu.VMEM((NVAR, CD, 640), BF),
             pltpu.VMEM((PLANE * 8, 128), F32),
             pltpu.VMEM((PLANE, 8, 128), BF),
@@ -542,9 +500,8 @@
             pltpu.VMEM((NLAT, 2, 128), F32),
             dma((9,)),
         ]
-        + [dma((PLANE,)), dma((PLANE,))] * 2
-        + [dma((2, NVAR)), dma((2, NVAR))]
-        + [dma((PLANE,)), dma((PLANE,))] * 3,
+        + [dma((1,)), dma((NLAT,))]
+        + [dma((1,)), dma((1,))] * 5,
         compiler_params=pltpu.CompilerParams(
             collective_id=0, has_side_effects=True, vmem_limit_bytes=32 * 1024 * 1024
         ),

time: 60 us -> 57.6 us (0.960)
  Pallas kernels: 59.2 us -> 56.9 us
    pallas_call x1, Pallas kernels: 58.3 us -> 55.9 us  [body(): pl.pallas_call(lambda *refs: kernel(total_area, *refs), out_shape=(jax.Sh...]
where the time goes in v3:
time: 57.6 us; the launch traced here: 57.5 us
  Pallas kernels  56.9 us (99%)
  between operations  0.64 us (1%)
    pallas_call x1, Pallas kernels, body(): pl.pallas_call(lambda *refs: kernel(total_area, *refs), out_shape=(jax.Sh...  55.9 us

profile of v3, /device:TPU:1, one launch (start us, length us, event | category | flops | bytes accessed | tf_op | source)
XLA Modules:
  0.0 57.5 jit_solution(594818842894675897)
XLA Ops:
  0.6 55.9 %spectral_layer.1 = (bf16[1,32,96,128]{3,2,1,0:T(8,128)(2,1)S(1)}, f32[32,2,128]{2,1,0:T(2,128)S(1)}) custom-call(bf16[1,32,96,128]{3,2,1,0:T(8,128)(2,1)} %refs_0_.1, bf16[1024,256]{1,0:T(8,128)(2,1)} %constant.10.clone.refs_1_, bf16[256,768]{1,0:T(8,128)(2,1)} %constant.11.clone.refs_2_, bf16[768,256]{1,0:T(8,128)(2,1)} %constant.12.clone.refs_3_, ...), custom_call_target="tpu_custom_call" | custom-call | tf_op jit(solution)/shard_map/spectral_layer/pallas_call | solution.py:469
  56.6 0.9 %finish.1 = (bf16[1,32,96,128]{3,2,1,0:T(8,128)(2,1)}, f32[1,32,96]{2,1,0:T(8,128)}, f32[32]{0:T(128)}) custom-call(bf16[1,32,96,128]{3,2,1,0:T(8,128)(2,1)S(1)} %get-tuple-element.5.field, f32[32,2,128]{2,1,0:T(2,128)S(1)} %get-tuple-element.6.stats), custom_call_target="tpu_custom_call" | custom-call | tf_op jit(solution)/shard_map/finish/pallas_call | solution.py:510

commit v4 on v3

--- a/solution.py
+++ b/solution.py
@@ -20,6 +20,10 @@
 RD = LAT // NLAT
 ND = LON // NLON
 JO = MLAT // PLANE
+CH = CD // 2
+PIECES = 4
+PIECE = CH // PIECES
+PITCH = PLANE * 6 + 8
 MESH = pl.DeviceIdType.MESH
 TAIL_AT = 0.23
 TAIL = (
@@ -76,8 +80,8 @@
     forward[:, 0:3, 1] = sine.reshape(PLANE, JO, LAT)
     forward[:, 3:6, 0] = -sine.reshape(PLANE, JO, LAT)
     forward[:, 3:6, 1] = cosine.reshape(PLANE, JO, LAT)
-    qtab = forward.reshape(PLANE * 8, 2 * LAT)
-    rtab = qtab.T
+    rtab = forward.reshape(PLANE * 8, 2 * LAT).T
+    qtab = forward[:, :6].reshape(PLANE * 6, 2, NLAT, RD).transpose(2, 0, 1, 3).reshape(NLAT, PLANE * 6, 2 * RD)
     area = np.cos(np.pi * ((r + 0.5) / LAT - 0.5))
     gtab = np.broadcast_to(area.reshape(NLAT, 1, RD), (NLAT, 8, RD))
     bf = lambda t: np.ascontiguousarray(t).astype(jnp.bfloat16)
@@ -125,11 +129,13 @@
     wov,
     bcol,
     xin,
-    lv,
-    sbuf,
-    srecv,
-    xf,
-    xall,
+    ss,
+    sa,
+    sb,
+    ra,
+    rb,
+    xa,
+    xb,
     mf,
     mbuf,
     mrecv,
@@ -174,10 +180,12 @@
         pltpu.make_async_copy(src, dst, load_sem.at[i])
         for i, (src, dst) in enumerate(
             [
-                (state.at[0], st),
+                (state.at[0, pl.ds(CH * (1 - core), CH)], st.at[1]),
+                (state.at[0, pl.ds(CH * core, CH)], st.at[0]),
+                (etab.at[pl.ds(b * ND, ND)], ev.at[pl.ds(0, ND)]),
+                (etab.at[pl.ds((b + 1 - 2 * core) * ND, ND)], ev.at[pl.ds(ND, ND)]),
+                (qtab.at[a], qv),
                 (bias, bcol.at[0:2]),
-                (etab, ev),
-                (qtab, qv),
                 (win, wiv),
                 (wout, wov),
                 (rtab, rv),
@@ -187,6 +195,7 @@
         )
     ]
     loads[0].start()
+    loads[1].start()
     scope("greet")
     barrier = pltpu.get_barrier_semaphore()
     for peer in PEERS:
@@ -196,7 +205,7 @@
     for d in far:
         pl.semaphore_signal(barrier, inc=1, device_id={"var": vars_[d]}, device_id_type=MESH)
 
-    for load in loads[1:]:
+    for load in loads[2:]:
         load.start()
     mf[...] = jnp.zeros_like(mf)
     zst[...] = jnp.zeros_like(zst)
@@ -210,126 +219,148 @@
         some = ref.at[pl.ds(0, PLANE - 1)]
         pltpu.make_async_copy(some, some, sem.at[0]).wait()
 
-    def copy1(src, dst, band, to):
+    scope("send1")
+    for i in range(PIECES):
+        pltpu.make_async_remote_copy(
+            src_ref=st.at[1, pl.ds(i * PIECE, PIECE)],
+            dst_ref=xin.at[pl.ds(i * PIECE, PIECE)],
+            send_sem=s1.at[0],
+            recv_sem=r1.at[i],
+            device_id={"lon": y * 2 + cores[1]},
+            device_id_type=MESH,
+        ).start()
+    loads[5].wait()
+    turned = jnp.transpose(bcol[...])
+    for load in loads[1:5]:
+        load.wait()
+
+    for i in range(PIECES):
+        scope(f"dft{i}")
+        some = xin.at[pl.ds(i * PIECE, PIECE)]
+        pltpu.make_async_copy(some, some, r1.at[i]).wait()
+        chans = slice(i * PIECE, (i + 1) * PIECE)
+        both = jnp.concatenate([st[0, chans], xin[chans]], axis=2).reshape(PIECE * RD, 2 * ND)
+        lon = jnp.dot(both, ev[...], preferred_element_type=F32).astype(BF)
+        for c in range(0, PIECE, 2):
+            one, two = lon[c * RD : (c + 1) * RD], lon[(c + 1) * RD : (c + 2) * RD]
+            pair = jnp.concatenate(
+                [
+                    jnp.concatenate([one[:, 0:128], two[:, 0:128]], axis=1),
+                    jnp.concatenate([one[:, 128:256], two[:, 128:256]], axis=1),
+                ],
+                axis=0,
+            )
+            spec = jnp.dot(qv[...], pair, preferred_element_type=F32)
+            at = (i * PIECE + c) * PITCH
+            ss[at : at + PLANE * 6, :] = spec[:, 0:128]
+            ss[at + PITCH : at + PITCH + PLANE * 6, :] = spec[:, 128:256]
+
+    lane = lax.broadcasted_iota(jnp.int32, (CH, 128), 1)
+    low, high = lane < 32, lane >= 96
+    second = jnp.logical_and(lane >= 32, lane < 64)
+
+    def pack(slot):
+        t = [ss[pl.ds(slot * 6 + i, CH, stride=PITCH), :] for i in range(6)]
+        up_r, half_r = pltpu.roll(t[2], 96, 1), pltpu.roll(t[2], 64, 1)
+        up_i, half_i = pltpu.roll(t[5], 96, 1), pltpu.roll(t[5], 64, 1)
+        p0, p1 = jnp.where(high, up_r, t[0]), jnp.where(high, half_r, t[1])
+        p2, p3 = jnp.where(high, up_i, t[3]), jnp.where(high, half_i, t[4])
+        p4 = jnp.where(low, half_r, jnp.where(second, up_i, 0.0))
+        sa[slot] = jnp.concatenate([p0, p2, p4], axis=1).astype(BF)
+        sb[slot] = jnp.concatenate([p1, p3], axis=1).astype(BF)
+
+    def copy2(src_ref, dst_ref, part, peer):
+        to, slot = plane(peer)
         return pltpu.make_async_remote_copy(
-            src_ref=st.at[src],
-            dst_ref=xin.at[dst],
-            send_sem=s1.at[0],
-            recv_sem=r1.at[band],
+            src_ref=src_ref.at[slot],
+            dst_ref=dst_ref.at[me],
+            send_sem=s2.at[part],
+            recv_sem=r2.at[part],
             device_id=to,
             device_id_type=MESH,
         )
 
-    scope("send1")
+    scope("pack")
     for peer in PEERS:
-        to, slot = plane(peer)
-        copy1(slot, me, a, to).start()
-    xin[me] = st[me]
-    scope("wait1")
-    loads[1].wait()
-    turned = jnp.transpose(bcol[...])
+        pack(plane(peer)[1])
+        copy2(sa, ra, 0, peer).start()
+    pack(me)
+    for peer in PEERS:
+        copy2(sb, rb, 1, peer).start()
+    ra[me] = sa[me]
+    rb[me] = sb[me]
     bias_r = jnp.broadcast_to(turned[:, 0:1], (256, 128))
     bias_i = jnp.broadcast_to(turned[:, 1:2], (256, 128))
-    loads[2].wait()
-    for da in (0, 1, 3, 2):
-        pa = lats[da]
-
-        some = xin.at[pl.ds(0, NLON if da else NLON - 1)]
-        pltpu.make_async_copy(some, some, r1.at[pa]).wait()
-        rows = jnp.concatenate([xin[(i % 2) * 16 + pa * 4 + i // 2] for i in range(NLON)], axis=1)
-        lv[pa] = jnp.dot(rows, ev[...], preferred_element_type=F32).astype(BF)
-
-    scope("fwd")
-    loads[3].wait()
-    lon = lv[...].reshape(LAT, 256)
-    spec = jnp.dot(qv[:, 0:LAT], lon[:, 0:128], preferred_element_type=F32)
-    spec += jnp.dot(qv[:, LAT : 2 * LAT], lon[:, 128:256], preferred_element_type=F32)
-    sbuf[...] = spec.reshape(PLANE, 8, 128).astype(BF)
-
-    def copy2(src, dst, to):
-        return pltpu.make_async_remote_copy(
-            src_ref=sbuf.at[src],
-            dst_ref=srecv.at[dst],
-            send_sem=s2.at[0],
-            recv_sem=r2.at[0],
-            device_id=to,
-            device_id_type=MESH,
-        )
-
-    scope("send2")
-    for peer in PEERS:
-        to, slot = plane(peer)
-        copy2(slot, me, to).start()
-    srecv[me] = sbuf[me]
-
-    scope("wait2")
-    whole(srecv, r2)
-    scope("pack")
-    xf[...] = srecv[...].astype(F32).reshape(PLANE * 8, 128)
-    t = [xf[pl.ds(i, PLANE, stride=8), :] for i in range(6)]
-    lane = lax.broadcasted_iota(jnp.int32, (PLANE, 128), 1)
-    low, high = lane < 32, lane >= 96
-    second = jnp.logical_and(lane >= 32, lane < 64)
-
-    def packed(t0, t1, t2):
-        up, half = pltpu.roll(t2, 96, 1), pltpu.roll(t2, 64, 1)
-        return jnp.where(high, up, t0), jnp.where(high, half, t1), up, half
-
-    p0, p1, _, last_r = packed(*t[0:3])
-    p2, p3, last_i, _ = packed(*t[3:6])
-    p4 = jnp.where(low, last_r, jnp.where(second, last_i, 0.0))
-    xall[v] = jnp.concatenate([p0, p1, p2, p3, p4], axis=1).astype(BF)
-    for d in far:
-        pltpu.make_async_remote_copy(
-            src_ref=xall.at[v],
-            dst_ref=xall.at[v],
-            send_sem=s3.at[0],
-            recv_sem=r3.at[0],
-            device_id={"var": vars_[d]},
-            device_id_type=MESH,
-        ).start()
+
+    def whole_at(ref, sem):
+        some = ref.at[pl.ds(0, PLANE - 1)]
+        pltpu.make_async_copy(some, some, sem).wait()
+
+    def others(ref, sem):
+        some = ref.at[pl.ds(0, NVAR - 1)]
+        return pltpu.make_async_copy(some, some, sem)
+
+    for part, (got, every) in enumerate(((ra, xa), (rb, xb))):
+        scope(f"wait2_{part}")
+        whole_at(got, r2.at[part])
+        scope(f"sum_{part}")
+        for half in range(2):
+            total = got[half * CH].astype(F32)
+            for i in range(1, CH):
+                total += got[half * CH + i].astype(F32)
+            every[v, half * CH : (half + 1) * CH] = total.astype(BF)
+        for d in far:
+            pltpu.make_async_remote_copy(
+                src_ref=every.at[v],
+                dst_ref=every.at[v],
+                send_sem=s3.at[part],
+                recv_sem=r3.at[part],
+                device_id={"var": vars_[d]},
+                device_id_type=MESH,
+            ).start()
 
     scope("wait3")
-    loads[4].wait()
-    loads[5].wait()
-    others = xall.at[pl.ds(0, NVAR - 1)]
-    pltpu.make_async_copy(others, others, r3.at[0]).wait()
-    scope("mix")
-    every = xall[...].reshape(NVAR * CD, 640)
-
-    def combined(g, half):
-        re = g[:half, 0:256] - g[half:, 256:512]
-        im = g[half:, 0:256] + g[:half, 256:512]
-        gr, gi = g[:half, 512:640], g[half:, 512:640]
-        which = lax.broadcasted_iota(jnp.int32, (half, 128), 1) < 32
-        last = jnp.where(which, gr - pltpu.roll(gi, 96, 1), gr + pltpu.roll(gi, 32, 1))
-        return re, im, last, which
-
-    g = jnp.dot(wiv[...].reshape(512, 256), every, preferred_element_type=F32)
-    re, im, last, which = combined(g, 256)
-    wide_r = jnp.concatenate([bias_r, bias_r], axis=1)
-    wide_i = jnp.concatenate([bias_i, bias_i], axis=1)
-    hidden = jnp.concatenate(
-        [re + wide_r, im + wide_i, last + jnp.where(which, bias_r, bias_i)], axis=1
-    )
-    hidden = jnp.maximum(hidden, 0.0).astype(BF)
+    for load in loads[6:8]:
+        load.wait()
     first = pl.multiple_of(v * CD, CD)
     own = jnp.concatenate([wov[0, pl.ds(first, CD), :], wov[1, pl.ds(first, CD), :]], axis=0)
-    g = jnp.dot(own, hidden, preferred_element_type=F32)
-    re, im, last, _ = combined(g, CD)
+
+    def combined(g, half):
+        re = g[:half, 0:128] - g[half:, 128:256]
+        im = g[half:, 0:128] + g[:half, 128:256]
+        if g.shape[1] == 256:
+            return re, im
+        gr, gi = g[:half, 256:384], g[half:, 256:384]
+        which = lax.broadcasted_iota(jnp.int32, (half, 128), 1) < 32
+        return re, im, jnp.where(which, gr - pltpu.roll(gi, 96, 1), gr + pltpu.roll(gi, 32, 1))
+
+    def mixed(every, part):
+        others(every, r3.at[part]).wait()
+        scope(f"mix_{part}")
+        g = jnp.dot(wiv[...].reshape(512, 256), every[...].reshape(256, -1), preferred_element_type=F32)
+        tiles = combined(g, 256)
+        which = lax.broadcasted_iota(jnp.int32, (256, 128), 1) < 32
+        biases = (bias_r, bias_i, jnp.where(which, bias_r, bias_i))
+        hidden = jnp.concatenate([t + c for t, c in zip(tiles, biases)], axis=1)
+        hidden = jnp.maximum(hidden, 0.0).astype(BF)
+        return combined(jnp.dot(own, hidden, preferred_element_type=F32), CD)
+
+    re0, im0, last = mixed(xa, 0)
+    scope("wait3_1")
+    re1, im1 = mixed(xb, 1)
     lane = lax.broadcasted_iota(jnp.int32, (CD, 128), 1)
     sel = [lane < 32, lane < 64]
     t2 = jnp.where(
         sel[0],
-        pltpu.roll(re[:, 0:128], 32, 1),
-        jnp.where(sel[1], pltpu.roll(re[:, 128:256], 64, 1), pltpu.roll(last, 64, 1)),
+        pltpu.roll(re0, 32, 1),
+        jnp.where(sel[1], pltpu.roll(re1, 64, 1), pltpu.roll(last, 64, 1)),
     )
     t5 = jnp.where(
         sel[0],
-        pltpu.roll(im[:, 0:128], 32, 1),
-        jnp.where(sel[1], pltpu.roll(im[:, 128:256], 64, 1), pltpu.roll(last, 32, 1)),
+        pltpu.roll(im0, 32, 1),
+        jnp.where(sel[1], pltpu.roll(im1, 64, 1), pltpu.roll(last, 32, 1)),
     )
-    for i, tile in enumerate([re[:, 0:128], re[:, 128:256], t2, im[:, 0:128], im[:, 128:256], t5]):
+    for i, tile in enumerate([re0, re1, t2, im0, im1, t5]):
         mf[pl.ds(i, PLANE, stride=8), :] = tile
     mbuf[...] = mf[...].reshape(PLANE, 8, 128).astype(BF)
 
@@ -349,7 +380,7 @@
         copy4(slot, me, to).start()
     mrecv[me] = mbuf[me]
     scope("wait4")
-    for load in loads[6:]:
+    for load in loads[8:]:
         load.wait()
     whole(mrecv, r4)
     scope("back")
@@ -431,9 +462,11 @@
     stats[me] = zst[a]
     scope("wait5")
 
-    whole(st, s1)
-    whole(sbuf, s2)
-    pltpu.make_async_copy(others, others, s3.at[0]).wait()
+    pltpu.make_async_copy(xin, xin, s1.at[0]).wait()
+    whole_at(sa, s2.at[0])
+    whole_at(sb, s2.at[1])
+    others(xa, s3.at[0]).wait()
+    others(xb, s3.at[1]).wait()
     whole(mbuf, s4)
     whole(fs, s5)
     whole(stats, s6)
@@ -475,21 +508,23 @@
         in_specs=[hbm] * 9,
         out_specs=(vmem, vmem),
         scratch_shapes=[
-            pltpu.VMEM((CD, RD, ND), BF),
-            pltpu.VMEM((LON, 256), BF),
-            pltpu.VMEM((256, 2 * LAT), BF),
+            pltpu.VMEM((2, CH, RD, ND), BF),
+            pltpu.VMEM((2 * ND, 256), BF),
+            pltpu.VMEM((PLANE * 6, 2 * RD), BF),
             pltpu.VMEM((2 * LAT, 256), BF),
             pltpu.VMEM((4, 256, 256), BF),
             pltpu.VMEM((NLAT, 8, RD), F32),
             pltpu.VMEM((2, 256, 256), BF),
             pltpu.VMEM((2, 256, 256), BF),
             pltpu.VMEM((128, 256), F32),
-            pltpu.VMEM((PLANE, RD, ND), BF),
-            pltpu.VMEM((NLAT, RD, 256), BF),
-            pltpu.VMEM((PLANE, 8, 128), BF),
-            pltpu.VMEM((PLANE, 8, 128), BF),
-            pltpu.VMEM((PLANE * 8, 128), F32),
-            pltpu.VMEM((NVAR, CD, 640), BF),
+            pltpu.VMEM((CH, RD, ND), BF),
+            pltpu.VMEM((CH * PITCH, 128), F32),
+            pltpu.VMEM((PLANE, CH, 384), BF),
+            pltpu.VMEM((PLANE, CH, 256), BF),
+            pltpu.VMEM((PLANE, CH, 384), BF),
+            pltpu.VMEM((PLANE, CH, 256), BF),
+            pltpu.VMEM((NVAR, CD, 384), BF),
+            pltpu.VMEM((NVAR, CD, 256), BF),
             pltpu.VMEM((PLANE * 8, 128), F32),
             pltpu.VMEM((PLANE, 8, 128), BF),
             pltpu.VMEM((PLANE, 8, 128), BF),
@@ -498,10 +533,10 @@
             pltpu.VMEM((NLAT, RD, 128), F32),
             pltpu.VMEM((NLAT, RD, 128), F32),
             pltpu.VMEM((NLAT, 2, 128), F32),
-            dma((9,)),
+            dma((11,)),
         ]
-        + [dma((1,)), dma((NLAT,))]
-        + [dma((1,)), dma((1,))] * 5,
+        + [dma((1,)), dma((PIECES,)), dma((2,)), dma((2,)), dma((2,)), dma((2,))]
+        + [dma((1,)), dma((1,))] * 3,
         compiler_params=pltpu.CompilerParams(
             collective_id=0, has_side_effects=True, vmem_limit_bytes=32 * 1024 * 1024
         ),

time: 57.6 us -> 53.8 us (0.934)
  Pallas kernels: 56.9 us -> 53.1 us
    pallas_call x1, Pallas kernels: 55.9 us -> 52.2 us  [body(): pl.pallas_call(lambda *refs: kernel(total_area, *refs), out_shape=(jax.Sh...]
where the time goes in v4:
time: 53.8 us; the launch traced here: 53.7 us
  Pallas kernels  53.1 us (99%)
  between operations  0.64 us (1%)
    pallas_call x1, Pallas kernels, body(): pl.pallas_call(lambda *refs: kernel(total_area, *refs), out_shape=(jax.Sh...  52.2 us

profile of v4, /device:TPU:1, one launch (start us, length us, event | category | flops | bytes accessed | tf_op | source)
XLA Modules:
  0.0 53.7 jit_solution(3409944157357473975)
XLA Ops:
  0.6 52.2 %spectral_layer.1 = (bf16[1,32,96,128]{3,2,1,0:T(8,128)(2,1)S(1)}, f32[32,2,128]{2,1,0:T(2,128)S(1)}) custom-call(bf16[1,32,96,128]{3,2,1,0:T(8,128)(2,1)} %refs_0_.1, bf16[1024,256]{1,0:T(8,128)(2,1)} %constant.10.clone.refs_1_, bf16[4,192,192]{2,1,0:T(8,128)(2,1)} %constant.11.clone.refs_2_, bf16[768,256]{1,0:T(8,128)(2,1)} %constant.12.clone.refs_3_, ...), custom_call_target="tpu_custom_call" | custom-call | tf_op jit(solution)/shard_map/spectral_layer/pallas_call | solution.py:502
  52.8 0.9 %finish.1 = (bf16[1,32,96,128]{3,2,1,0:T(8,128)(2,1)}, f32[1,32,96]{2,1,0:T(8,128)}, f32[32]{0:T(128)}) custom-call(bf16[1,32,96,128]{3,2,1,0:T(8,128)(2,1)S(1)} %get-tuple-element.5.field, f32[32,2,128]{2,1,0:T(2,128)S(1)} %get-tuple-element.6.stats), custom_call_target="tpu_custom_call" | custom-call | tf_op jit(solution)/shard_map/finish/pallas_call | solution.py:545

commit v5 on v4

--- a/solution.py
+++ b/solution.py
@@ -21,7 +21,7 @@
 ND = LON // NLON
 JO = MLAT // PLANE
 CH = CD // 2
-PIECES = 4
+PIECES = 2
 PIECE = CH // PIECES
 PITCH = PLANE * 6 + 8
 MESH = pl.DeviceIdType.MESH
@@ -132,10 +132,13 @@
     ss,
     sa,
     sb,
+    sc,
     ra,
     rb,
+    rc,
     xa,
     xb,
+    xc,
     mf,
     mbuf,
     mrecv,
@@ -213,6 +216,7 @@
     acc2[...] = jnp.zeros_like(acc2)
     scope("barrier")
     loads[0].wait()
+    scope("barrier2")
     pl.semaphore_wait(barrier, PLANE - 1 + NVAR - 1)
 
     def whole(ref, sem):
@@ -266,8 +270,9 @@
         p0, p1 = jnp.where(high, up_r, t[0]), jnp.where(high, half_r, t[1])
         p2, p3 = jnp.where(high, up_i, t[3]), jnp.where(high, half_i, t[4])
         p4 = jnp.where(low, half_r, jnp.where(second, up_i, 0.0))
-        sa[slot] = jnp.concatenate([p0, p2, p4], axis=1).astype(BF)
+        sa[slot] = jnp.concatenate([p0, p2], axis=1).astype(BF)
         sb[slot] = jnp.concatenate([p1, p3], axis=1).astype(BF)
+        sc[slot] = (p4[0:8] + pltpu.roll(p4[8:16], 64, 1)).astype(BF)
 
     def copy2(src_ref, dst_ref, part, peer):
         to, slot = plane(peer)
@@ -281,14 +286,19 @@
         )
 
     scope("pack")
-    for peer in PEERS:
-        pack(plane(peer)[1])
-        copy2(sa, ra, 0, peer).start()
-    pack(me)
+    for i in range(0, len(PEERS), 8):
+        for peer in PEERS[i : i + 8]:
+            pack(plane(peer)[1])
+        for peer in PEERS[i : i + 8]:
+            copy2(sa, ra, 0, peer).start()
     for peer in PEERS:
         copy2(sb, rb, 1, peer).start()
+    for peer in PEERS:
+        copy2(sc, rc, 2, peer).start()
+    pack(me)
     ra[me] = sa[me]
     rb[me] = sb[me]
+    rc[me] = sc[me]
     bias_r = jnp.broadcast_to(turned[:, 0:1], (256, 128))
     bias_i = jnp.broadcast_to(turned[:, 1:2], (256, 128))
 
@@ -300,7 +310,7 @@
         some = ref.at[pl.ds(0, NVAR - 1)]
         return pltpu.make_async_copy(some, some, sem)
 
-    for part, (got, every) in enumerate(((ra, xa), (rb, xb))):
+    for part, (got, every) in enumerate(((ra, xa), (rb, xb), (rc, xc))):
         scope(f"wait2_{part}")
         whole_at(got, r2.at[part])
         scope(f"sum_{part}")
@@ -308,7 +318,8 @@
             total = got[half * CH].astype(F32)
             for i in range(1, CH):
                 total += got[half * CH + i].astype(F32)
-            every[v, half * CH : (half + 1) * CH] = total.astype(BF)
+            rows = got.shape[1]
+            every[v, half * rows : (half + 1) * rows] = total.astype(BF)
         for d in far:
             pltpu.make_async_remote_copy(
                 src_ref=every.at[v],
@@ -326,42 +337,47 @@
     own = jnp.concatenate([wov[0, pl.ds(first, CD), :], wov[1, pl.ds(first, CD), :]], axis=0)
 
     def combined(g, half):
-        re = g[:half, 0:128] - g[half:, 128:256]
-        im = g[half:, 0:128] + g[:half, 128:256]
         if g.shape[1] == 256:
-            return re, im
-        gr, gi = g[:half, 256:384], g[half:, 256:384]
+            return g[:half, 0:128] - g[half:, 128:256], g[half:, 0:128] + g[:half, 128:256]
         which = lax.broadcasted_iota(jnp.int32, (half, 128), 1) < 32
-        return re, im, jnp.where(which, gr - pltpu.roll(gi, 96, 1), gr + pltpu.roll(gi, 32, 1))
+        gr, gi = g[:half], g[half:]
+        return (jnp.where(which, gr - pltpu.roll(gi, 96, 1), gr + pltpu.roll(gi, 32, 1)),)
 
     def mixed(every, part):
         others(every, r3.at[part]).wait()
         scope(f"mix_{part}")
-        g = jnp.dot(wiv[...].reshape(512, 256), every[...].reshape(256, -1), preferred_element_type=F32)
+        if every is xc:
+            folded = xc[...].astype(F32).reshape(2 * NVAR, 8, 128)
+            beside = pltpu.roll(folded, 64, 2)
+            rows = jnp.stack([folded, beside], axis=1).reshape(256, 128).astype(BF)
+        else:
+            rows = every[...].reshape(256, -1)
+        g = jnp.dot(wiv[...].reshape(512, 256), rows, preferred_element_type=F32)
         tiles = combined(g, 256)
         which = lax.broadcasted_iota(jnp.int32, (256, 128), 1) < 32
-        biases = (bias_r, bias_i, jnp.where(which, bias_r, bias_i))
+        biases = (bias_r, bias_i) if len(tiles) == 2 else (jnp.where(which, bias_r, bias_i),)
         hidden = jnp.concatenate([t + c for t, c in zip(tiles, biases)], axis=1)
         hidden = jnp.maximum(hidden, 0.0).astype(BF)
         return combined(jnp.dot(own, hidden, preferred_element_type=F32), CD)
 
-    re0, im0, last = mixed(xa, 0)
+    lane = lax.broadcasted_iota(jnp.int32, (CD, 128), 1)
+
+    def put(i, tile):
+        mf[pl.ds(i, PLANE, stride=8), :] = tile
+
+    re0, im0 = mixed(xa, 0)
+    put(0, re0)
+    put(3, im0)
     scope("wait3_1")
     re1, im1 = mixed(xb, 1)
-    lane = lax.broadcasted_iota(jnp.int32, (CD, 128), 1)
-    sel = [lane < 32, lane < 64]
-    t2 = jnp.where(
-        sel[0],
-        pltpu.roll(re0, 32, 1),
-        jnp.where(sel[1], pltpu.roll(re1, 64, 1), pltpu.roll(last, 64, 1)),
-    )
-    t5 = jnp.where(
-        sel[0],
-        pltpu.roll(im0, 32, 1),
-        jnp.where(sel[1], pltpu.roll(im1, 64, 1), pltpu.roll(last, 32, 1)),
-    )
-    for i, tile in enumerate([re0, re1, t2, im0, im1, t5]):
-        mf[pl.ds(i, PLANE, stride=8), :] = tile
+    put(1, re1)
+    put(4, im1)
+    kept_r = jnp.where(lane < 32, pltpu.roll(re0, 32, 1), pltpu.roll(re1, 64, 1))
+    kept_i = jnp.where(lane < 32, pltpu.roll(im0, 32, 1), pltpu.roll(im1, 64, 1))
+    scope("wait3_2")
+    (last,) = mixed(xc, 2)
+    put(2, jnp.where(lane < 64, kept_r, pltpu.roll(last, 64, 1)))
+    put(5, jnp.where(lane < 64, kept_i, pltpu.roll(last, 32, 1)))
     mbuf[...] = mf[...].reshape(PLANE, 8, 128).astype(BF)
 
     def copy4(src, dst, to):
@@ -413,7 +429,7 @@
         copy5(slot, me, to).start()
 
     scope("gelu")
-    near = [c for c in CHIPS if ring(c[0]) + ring(c[1]) <= 2]
+    near = [c for c in CHIPS if ring(c[0]) + ring(c[1]) <= 1]
     for c in CHIPS:
         chip(*c)
         if c not in near:
@@ -465,8 +481,10 @@
     pltpu.make_async_copy(xin, xin, s1.at[0]).wait()
     whole_at(sa, s2.at[0])
     whole_at(sb, s2.at[1])
+    whole_at(sc, s2.at[2])
     others(xa, s3.at[0]).wait()
     others(xb, s3.at[1]).wait()
+    others(xc, s3.at[2]).wait()
     whole(mbuf, s4)
     whole(fs, s5)
     whole(stats, s6)
@@ -519,12 +537,15 @@
             pltpu.VMEM((128, 256), F32),
             pltpu.VMEM((CH, RD, ND), BF),
             pltpu.VMEM((CH * PITCH, 128), F32),
-            pltpu.VMEM((PLANE, CH, 384), BF),
             pltpu.VMEM((PLANE, CH, 256), BF),
-            pltpu.VMEM((PLANE, CH, 384), BF),
             pltpu.VMEM((PLANE, CH, 256), BF),
-            pltpu.VMEM((NVAR, CD, 384), BF),
+            pltpu.VMEM((PLANE, 8, 128), BF),
+            pltpu.VMEM((PLANE, CH, 256), BF),
+            pltpu.VMEM((PLANE, CH, 256), BF),
+            pltpu.VMEM((PLANE, 8, 128), BF),
             pltpu.VMEM((NVAR, CD, 256), BF),
+            pltpu.VMEM((NVAR, CD, 256), BF),
+            pltpu.VMEM((NVAR, CH, 128), BF),
             pltpu.VMEM((PLANE * 8, 128), F32),
             pltpu.VMEM((PLANE, 8, 128), BF),
             pltpu.VMEM((PLANE, 8, 128), BF),
@@ -535,7 +556,7 @@
             pltpu.VMEM((NLAT, 2, 128), F32),
             dma((11,)),
         ]
-        + [dma((1,)), dma((PIECES,)), dma((2,)), dma((2,)), dma((2,)), dma((2,))]
+        + [dma((1,)), dma((PIECES,)), dma((3,)), dma((3,)), dma((3,)), dma((3,))]
         + [dma((1,)), dma((1,))] * 3,
         compiler_params=pltpu.CompilerParams(
             collective_id=0, has_side_effects=True, vmem_limit_bytes=32 * 1024 * 1024

time: 53.8 us -> 49.7 us (0.924)
  Pallas kernels: 53.1 us -> 49 us
    pallas_call x1, Pallas kernels: 52.2 us -> 48.1 us  [body(): pl.pallas_call(lambda *refs: kernel(total_area, *refs), out_shape=(jax.Sh...]
where the time goes in v5:
time: 49.7 us; the launch traced here: 49.6 us
  Pallas kernels  49 us (99%)
  between operations  0.64 us (1%)
    pallas_call x1, Pallas kernels, body(): pl.pallas_call(lambda *refs: kernel(total_area, *refs), out_shape=(jax.Sh...  48.1 us

profile of v5, /device:TPU:1, one launch (start us, length us, event | category | flops | bytes accessed | tf_op | source)
XLA Modules:
  0.0 49.6 jit_solution(9664787521612601745)
XLA Ops:
  0.6 48.1 %spectral_layer.1 = (bf16[1,32,96,128]{3,2,1,0:T(8,128)(2,1)S(1)}, f32[32,2,128]{2,1,0:T(2,128)S(1)}) custom-call(bf16[1,32,96,128]{3,2,1,0:T(8,128)(2,1)} %refs_0_.1, bf16[1024,256]{1,0:T(8,128)(2,1)} %constant.10.clone.refs_1_, bf16[4,192,192]{2,1,0:T(8,128)(2,1)} %constant.11.clone.refs_2_, bf16[768,256]{1,0:T(8,128)(2,1)} %constant.12.clone.refs_3_, ...), custom_call_target="tpu_custom_call" | custom-call | tf_op jit(solution)/shard_map/spectral_layer/pallas_call | solution.py:520
  48.7 0.9 %finish.1 = (bf16[1,32,96,128]{3,2,1,0:T(8,128)(2,1)}, f32[1,32,96]{2,1,0:T(8,128)}, f32[32]{0:T(128)}) custom-call(bf16[1,32,96,128]{3,2,1,0:T(8,128)(2,1)S(1)} %get-tuple-element.5.field, f32[32,2,128]{2,1,0:T(2,128)S(1)} %get-tuple-element.6.stats), custom_call_target="tpu_custom_call" | custom-call | tf_op jit(solution)/shard_map/finish/pallas_call | solution.py:566

commit v6 on v5

--- a/solution.py
+++ b/solution.py
@@ -70,20 +70,20 @@
     full = np.zeros((256, LON), np.float32)
     full[:MLON] = weight * np.cos(angle.T)
     full[128 : 128 + MLON] = -weight * np.sin(angle.T)
-    htab = full.reshape(256, 4, 2 * ND).transpose(1, 0, 2)
+    htab = full.reshape(256, NLON, ND).transpose(1, 0, 2)
     r = np.arange(LAT)
     freqs = np.arange(MLAT) - MLAT // 2
     turn = 2.0 * np.pi / LAT * np.mod(freqs[:, None] * r[None, :], LAT)
     cosine, sine = np.cos(turn), np.sin(turn)
-    forward = np.zeros((PLANE, 8, 2, LAT), np.float32)
+    forward = np.zeros((PLANE, 6, 2, LAT), np.float32)
     forward[:, 0:3, 0] = cosine.reshape(PLANE, JO, LAT)
     forward[:, 0:3, 1] = sine.reshape(PLANE, JO, LAT)
     forward[:, 3:6, 0] = -sine.reshape(PLANE, JO, LAT)
     forward[:, 3:6, 1] = cosine.reshape(PLANE, JO, LAT)
-    rtab = forward.reshape(PLANE * 8, 2 * LAT).T
-    qtab = forward[:, :6].reshape(PLANE * 6, 2, NLAT, RD).transpose(2, 0, 1, 3).reshape(NLAT, PLANE * 6, 2 * RD)
+    qtab = forward.reshape(PLANE * 6, 2, NLAT, RD).transpose(2, 0, 1, 3).reshape(NLAT, PLANE * 6, 2 * RD)
+    rtab = qtab.transpose(0, 2, 1)
     area = np.cos(np.pi * ((r + 0.5) / LAT - 0.5))
-    gtab = np.broadcast_to(area.reshape(NLAT, 1, RD), (NLAT, 8, RD))
+    gtab = np.broadcast_to(area.reshape(NLAT, RD, 1), (NLAT, RD, 128))
     bf = lambda t: np.ascontiguousarray(t).astype(jnp.bfloat16)
     return (
         bf(etab),
@@ -107,7 +107,6 @@
 
 
 def kernel(
-    total_area,
     state,
     etab,
     qtab,
@@ -118,7 +117,8 @@
     bias,
     wout,
     field,
-    stats,
+    zrec,
+    erec,
     st,
     ev,
     qv,
@@ -139,14 +139,17 @@
     xa,
     xb,
     xc,
-    mf,
-    mbuf,
-    mrecv,
-    lbv,
+    ma,
+    mb,
+    mc,
+    ba,
+    bb,
+    bc,
     fs,
-    acc,
-    acc2,
-    zst,
+    zacc,
+    eacc,
+    zmsg,
+    emsg,
     load_sem,
     s1,
     r1,
@@ -160,6 +163,8 @@
     r5,
     s6,
     r6,
+    s7,
+    r7,
 ):
     v = lax.axis_index("var")
     a = lax.axis_index("lat")
@@ -191,9 +196,10 @@
                 (bias, bcol.at[0:2]),
                 (win, wiv),
                 (wout, wov),
-                (rtab, rv),
-                (htab, hv),
-                (gtab, gv),
+                (rtab.at[a], rv),
+                (htab.at[b], hv.at[:, pl.ds(0, ND)]),
+                (htab.at[b + 1 - 2 * core], hv.at[:, pl.ds(ND, ND)]),
+                (gtab.at[a], gv),
             ]
         )
     ]
@@ -210,18 +216,11 @@
 
     for load in loads[2:]:
         load.start()
-    mf[...] = jnp.zeros_like(mf)
-    zst[...] = jnp.zeros_like(zst)
-    acc[...] = jnp.zeros_like(acc)
-    acc2[...] = jnp.zeros_like(acc2)
+    zacc[...] = jnp.zeros_like(zacc)
     scope("barrier")
     loads[0].wait()
     scope("barrier2")
     pl.semaphore_wait(barrier, PLANE - 1 + NVAR - 1)
-
-    def whole(ref, sem):
-        some = ref.at[pl.ds(0, PLANE - 1)]
-        pltpu.make_async_copy(some, some, sem.at[0]).wait()
 
     scope("send1")
     for i in range(PIECES):
@@ -360,150 +359,161 @@
         hidden = jnp.maximum(hidden, 0.0).astype(BF)
         return combined(jnp.dot(own, hidden, preferred_element_type=F32), CD)
 
-    lane = lax.broadcasted_iota(jnp.int32, (CD, 128), 1)
-
-    def put(i, tile):
-        mf[pl.ds(i, PLANE, stride=8), :] = tile
-
-    re0, im0 = mixed(xa, 0)
-    put(0, re0)
-    put(3, im0)
-    scope("wait3_1")
-    re1, im1 = mixed(xb, 1)
-    put(1, re1)
-    put(4, im1)
-    kept_r = jnp.where(lane < 32, pltpu.roll(re0, 32, 1), pltpu.roll(re1, 64, 1))
-    kept_i = jnp.where(lane < 32, pltpu.roll(im0, 32, 1), pltpu.roll(im1, 64, 1))
-    scope("wait3_2")
-    (last,) = mixed(xc, 2)
-    put(2, jnp.where(lane < 64, kept_r, pltpu.roll(last, 64, 1)))
-    put(5, jnp.where(lane < 64, kept_i, pltpu.roll(last, 32, 1)))
-    mbuf[...] = mf[...].reshape(PLANE, 8, 128).astype(BF)
-
-    def copy4(src, dst, to):
+    def copy4(src_ref, dst_ref, part, peer):
+        to, slot = plane(peer)
         return pltpu.make_async_remote_copy(
-            src_ref=mbuf.at[src],
-            dst_ref=mrecv.at[dst],
-            send_sem=s4.at[0],
-            recv_sem=r4.at[0],
+            src_ref=src_ref.at[cores[peer[2]]],
+            dst_ref=dst_ref.at[me],
+            send_sem=s4.at[part],
+            recv_sem=r4.at[part],
             device_id=to,
             device_id_type=MESH,
         )
 
-    scope("send4")
-    for peer in PEERS:
-        to, slot = plane(peer)
-        copy4(slot, me, to).start()
-    mrecv[me] = mbuf[me]
-    scope("wait4")
+    def spread(part, src_ref, dst_ref):
+        scope(f"send4_{part}")
+        for peer in PEERS:
+            copy4(src_ref, dst_ref, part, peer).start()
+        dst_ref[me] = src_ref[core]
+
+    ma[...] = jnp.concatenate(mixed(xa, 0), axis=1).astype(BF).reshape(2, CH, 256)
+    spread(0, ma, ba)
+    scope("wait3_1")
+    mb[...] = jnp.concatenate(mixed(xb, 1), axis=1).astype(BF).reshape(2, CH, 256)
+    spread(1, mb, bb)
+    scope("wait3_2")
+    (last,) = mixed(xc, 2)
+    last = jnp.where(lax.broadcasted_iota(jnp.int32, (CD, 128), 1) < 64, last, 0.0).reshape(2, 2, 8, 128)
+    mc[...] = (last[:, 0] + pltpu.roll(last[:, 1], 64, 2)).astype(BF)
+    spread(2, mc, bc)
+
+    def put(owner, i, tile):
+        ss[pl.ds(owner * 6 + i, CH, stride=PITCH), :] = tile
+
+    for part, (got, i) in enumerate(((ba, 0), (bb, 1))):
+        scope(f"wait4_{part}")
+        whole_at(got, r4.at[part])
+        scope(f"unpack_{part}")
+        for o in range(PLANE):
+            tiles = got[o].astype(F32)
+            put(o, i, tiles[:, 0:128])
+            put(o, i + 3, tiles[:, 128:256])
+    scope("wait4_2")
     for load in loads[8:]:
         load.wait()
-    whole(mrecv, r4)
-    scope("back")
-    modes = mrecv[...].reshape(PLANE * 8, 128)
-    back_r = jnp.dot(rv[0:LAT, :], modes, preferred_element_type=F32)
-    back_i = jnp.dot(rv[LAT : 2 * LAT, :], modes, preferred_element_type=F32)
-    lbv[...] = jnp.concatenate([back_r, back_i], axis=1).astype(BF).reshape(NLAT, RD, 256)
-
-    def copy5(src, dst, to):
+    whole_at(bc, r4.at[2])
+    scope("unpack_2")
+    mid = lane < 64
+    for o in range(PLANE):
+        one, two, folded = ba[o].astype(F32), bb[o].astype(F32), bc[o].astype(F32)
+        end = jnp.concatenate([folded, pltpu.roll(folded, 64, 1)], axis=0)
+        for i, cols, shift in ((2, slice(0, 128), 64), (5, slice(128, 256), 32)):
+            start = jnp.where(low, pltpu.roll(one[:, cols], 32, 1), pltpu.roll(two[:, cols], 64, 1))
+            put(o, i, jnp.where(mid, start, pltpu.roll(end, shift, 1)))
+
+    column = lax.broadcasted_iota(jnp.int32, (RD, 128), 1)
+    for c in range(0, CH, 2):
+        if c % PIECE == 0:
+            scope(f"gelu{c}")
+        pair = jnp.concatenate(
+            [ss[(c + i) * PITCH : (c + i) * PITCH + PLANE * 6, :] for i in range(2)], axis=1
+        ).astype(BF)
+        back = jnp.dot(rv[...], pair, preferred_element_type=F32).astype(BF)
+        both = jnp.concatenate(
+            [jnp.concatenate([back[0:RD, at], back[RD:, at]], axis=1) for at in (slice(0, 128), slice(128, 256))],
+            axis=0,
+        )
+        act = gelu(jnp.dot(both, hv[...], preferred_element_type=F32))
+        square = act * act
+        for i in range(2):
+            mine, at = act[i * RD : (i + 1) * RD], c + i
+            field[0, core * CH + at] = mine[:, 0:128].astype(BF)
+            fs[at] = mine[:, 128:256].astype(BF)
+            total = jnp.sum(mine[:, 0:128] + mine[:, 128:256], axis=1, keepdims=True)
+            zacc[0:RD, :] += jnp.where(column == at, total, 0.0)
+            part = square[i * RD : (i + 1) * RD]
+            part = (part[:, 0:128] + part[:, 128:256]) * gv[...]
+            eacc[at] = jnp.sum(part.reshape(RD // 8, 8, 128), axis=0)
+        if (c + 2) % PIECE == 0:
+            first = c + 2 - PIECE
+            pltpu.make_async_remote_copy(
+                src_ref=fs.at[pl.ds(first, PIECE)],
+                dst_ref=field.at[0, pl.ds(core * CH + first, PIECE)],
+                send_sem=s5.at[0],
+                recv_sem=r5.at[0],
+                device_id={"lon": y * 2 + cores[1]},
+                device_id_type=MESH,
+            ).start()
+
+    scope("stats")
+    zmsg[...] = jnp.transpose(zacc[...])[0:CH]
+    ones = jnp.ones((8, 128), F32)
+    highest = dict(precision=lax.Precision.HIGHEST, preferred_element_type=F32)
+    flat = lax.dot_general(ones, eacc[...].reshape(CH * 8, 128), (((1,), (1,)), ((), ())), **highest)
+    channel = lax.div(lax.broadcasted_iota(jnp.int32, (128, 128), 0), 8) + core * CH
+    pick = jnp.where(channel == lax.broadcasted_iota(jnp.int32, (128, 128), 1), 1.0, 0.0)
+    emsg[...] = jnp.dot(flat, pick, **highest)[0:2]
+
+    def copy6(peer):
+        to, slot = plane(peer)
         return pltpu.make_async_remote_copy(
-            src_ref=fs.at[src],
-            dst_ref=field.at[0, dst],
-            send_sem=s5.at[0],
-            recv_sem=r5.at[0],
-            device_id=to,
-            device_id_type=MESH,
-        )
-
-    def chip(i, j):
-        pa, py = lats[i], ys[j]
-        act = gelu(jnp.dot(lbv[pa], hv[py], preferred_element_type=F32))
-        fs[slot_of(pa, py, 0)] = act[:, 0:128].astype(BF)
-        fs[slot_of(pa, py, 1)] = act[:, 128:256].astype(BF)
-        acc[pa] += act[:, 0:128] + act[:, 128:256]
-        square = act * act
-        acc2[pa] += square[:, 0:128] + square[:, 128:256]
-
-    def send5(peer):
-        to, slot = plane(peer)
-        copy5(slot, me, to).start()
-
-    scope("gelu")
-    near = [c for c in CHIPS if ring(c[0]) + ring(c[1]) <= 1]
-    for c in CHIPS:
-        chip(*c)
-        if c not in near:
-            send5((*c, 0))
-            send5((*c, 1))
-    chip(0, 0)
-    scope("stats")
-    ones = jnp.ones((8, 128), F32)
-    weighted = jnp.zeros((8, 128), F32)
-    for band in range(NLAT):
-        rowsum = lax.dot_general(
-            ones,
-            acc[band],
-            (((1,), (1,)), ((), ())),
-            precision=lax.Precision.HIGHEST,
-            preferred_element_type=F32,
-        )
-        zst[band, 0:1, 0:RD] = rowsum[0:1] * (1.0 / LON)
-        weighted += jnp.dot(
-            gv[band], acc2[band], precision=lax.Precision.HIGHEST, preferred_element_type=F32
-        )
-    total = jnp.sum(weighted, axis=1, keepdims=True)[0:1] * (1.0 / total_area)
-    mine = jnp.where(lax.broadcasted_iota(jnp.int32, (1, 128), 1) == me, total, 0.0)
-    for band in range(NLAT):
-        zst[band, 1:2, :] = mine
-
-    def copy6(src, dst, band, to):
-        return pltpu.make_async_remote_copy(
-            src_ref=zst.at[band],
-            dst_ref=stats.at[dst],
+            src_ref=emsg,
+            dst_ref=erec.at[me],
             send_sem=s6.at[0],
             recv_sem=r6.at[0],
             device_id=to,
             device_id_type=MESH,
         )
 
+    def copy7(peer):
+        to, _ = plane(peer)
+        return pltpu.make_async_remote_copy(
+            src_ref=zmsg,
+            dst_ref=zrec.at[core * 4 + y],
+            send_sem=s7.at[0],
+            recv_sem=r7.at[0],
+            device_id=to,
+            device_id_type=MESH,
+        )
+
     scope("send6")
     for peer in PEERS:
-        to, slot = plane(peer)
-        copy6(slot, me, lats[peer[0]], to).start()
-    for c in near:
-        send5((*c, 0))
-        send5((*c, 1))
-    send5((0, 0, 1))
-    field[0, me] = fs[me]
-    stats[me] = zst[a]
+        copy6(peer).start()
+    for peer in PEERS:
+        if peer[0] == 0:
+            copy7(peer).start()
+    zrec[core * 4 + y] = zmsg[...]
+    erec[me] = emsg[...]
     scope("wait5")
-
     pltpu.make_async_copy(xin, xin, s1.at[0]).wait()
-    whole_at(sa, s2.at[0])
-    whole_at(sb, s2.at[1])
-    whole_at(sc, s2.at[2])
-    others(xa, s3.at[0]).wait()
-    others(xb, s3.at[1]).wait()
-    others(xc, s3.at[2]).wait()
-    whole(mbuf, s4)
-    whole(fs, s5)
-    whole(stats, s6)
-    whole(field.at[0], r5)
-    whole(stats, r6)
+    for part, (sent, every, spreads) in enumerate(((sa, xa, ba), (sb, xb, bb), (sc, xc, bc))):
+        whole_at(sent, s2.at[part])
+        others(every, s3.at[part]).wait()
+        whole_at(spreads, s4.at[part])
+    half = fs.at[pl.ds(0, CH)]
+    pltpu.make_async_copy(half, half, s5.at[0]).wait()
+    pltpu.make_async_copy(half, half, r5.at[0]).wait()
+    scope("wait6")
+    whole_at(erec, s6.at[0])
+    seven = zrec.at[pl.ds(0, NLON - 1)]
+    pltpu.make_async_copy(seven, seven, s7.at[0]).wait()
+    pltpu.make_async_copy(seven, seven, r7.at[0]).wait()
+    whole_at(erec, r6.at[0])
     scope(None)
 
 
-def finish(field, stats, out, zonal, energy, zv, evec, sems):
+def finish(total_area, field, rows, sums, out, zonal, energy, zv, evec, sems):
     big = pltpu.make_async_copy(field, out, sems.at[0])
     big.start()
-    gathered = jnp.zeros((1, 128), F32)
-    for i in range(CD):
-        both = stats[i]
-        zv[0, i : i + 1, :] = both[0:1, 0:RD]
-        gathered += both[1:2, :]
-    evec[...] = gathered[0, 0:CD]
+    for half in range(2):
+        total = rows[half * 4] + rows[half * 4 + 1] + rows[half * 4 + 2] + rows[half * 4 + 3]
+        zv[0, half * CH : (half + 1) * CH, :] = total[:, 0:RD] * (1.0 / LON)
     small = pltpu.make_async_copy(zv, zonal, sems.at[1])
     small.start()
+    gathered = sums[0]
+    for i in range(1, PLANE):
+        gathered += sums[i]
+    evec[...] = gathered[0, 0:CD] * (1.0 / total_area)
     other = pltpu.make_async_copy(evec, energy, sems.at[2])
     other.start()
     big.wait()
@@ -517,21 +527,22 @@
     vmem = pl.BlockSpec(memory_space=pltpu.VMEM)
     dma = pltpu.SemaphoreType.DMA
     operands = (state, *(jnp.asarray(t) for t in tabs), weights_in, bias_in, weights_out)
-    field, stats = pl.pallas_call(
-        lambda *refs: kernel(total_area, *refs),
+    field, rows, sums = pl.pallas_call(
+        kernel,
         out_shape=(
             jax.ShapeDtypeStruct((1, CD, RD, ND), BF),
+            jax.ShapeDtypeStruct((NLON, CH, 128), F32),
             jax.ShapeDtypeStruct((PLANE, 2, 128), F32),
         ),
         in_specs=[hbm] * 9,
-        out_specs=(vmem, vmem),
+        out_specs=(vmem, vmem, vmem),
         scratch_shapes=[
             pltpu.VMEM((2, CH, RD, ND), BF),
             pltpu.VMEM((2 * ND, 256), BF),
             pltpu.VMEM((PLANE * 6, 2 * RD), BF),
-            pltpu.VMEM((2 * LAT, 256), BF),
-            pltpu.VMEM((4, 256, 256), BF),
-            pltpu.VMEM((NLAT, 8, RD), F32),
+            pltpu.VMEM((2 * RD, PLANE * 6), BF),
+            pltpu.VMEM((256, 2 * ND), BF),
+            pltpu.VMEM((RD, 128), F32),
             pltpu.VMEM((2, 256, 256), BF),
             pltpu.VMEM((2, 256, 256), BF),
             pltpu.VMEM((128, 256), F32),
@@ -546,17 +557,21 @@
             pltpu.VMEM((NVAR, CD, 256), BF),
             pltpu.VMEM((NVAR, CD, 256), BF),
             pltpu.VMEM((NVAR, CH, 128), BF),
-            pltpu.VMEM((PLANE * 8, 128), F32),
+            pltpu.VMEM((2, CH, 256), BF),
+            pltpu.VMEM((2, CH, 256), BF),
+            pltpu.VMEM((2, 8, 128), BF),
+            pltpu.VMEM((PLANE, CH, 256), BF),
+            pltpu.VMEM((PLANE, CH, 256), BF),
             pltpu.VMEM((PLANE, 8, 128), BF),
-            pltpu.VMEM((PLANE, 8, 128), BF),
-            pltpu.VMEM((NLAT, RD, 256), BF),
-            pltpu.VMEM((PLANE, RD, ND), BF),
-            pltpu.VMEM((NLAT, RD, 128), F32),
-            pltpu.VMEM((NLAT, RD, 128), F32),
-            pltpu.VMEM((NLAT, 2, 128), F32),
-            dma((11,)),
+            pltpu.VMEM((CH, RD, ND), BF),
+            pltpu.VMEM((128, 128), F32),
+            pltpu.VMEM((CH, 8, 128), F32),
+            pltpu.VMEM((CH, 128), F32),
+            pltpu.VMEM((2, 128), F32),
+            dma((12,)),
         ]
         + [dma((1,)), dma((PIECES,)), dma((3,)), dma((3,)), dma((3,)), dma((3,))]
+        + [dma((3,)), dma((3,))]
         + [dma((1,)), dma((1,))] * 3,
         compiler_params=pltpu.CompilerParams(
             collective_id=0, has_side_effects=True, vmem_limit_bytes=32 * 1024 * 1024
@@ -564,13 +579,13 @@
         name="spectral_layer",
     )(*(pltpu.with_memory_space_constraint(x, pltpu.HBM) for x in operands))
     return pl.pallas_call(
-        finish,
+        lambda *refs: finish(total_area, *refs),
         out_shape=(
             jax.ShapeDtypeStruct((1, CD, RD, ND), BF),
             jax.ShapeDtypeStruct((1, CD, RD), F32),
             jax.ShapeDtypeStruct((CD,), F32),
         ),
-        in_specs=[vmem, vmem],
+        in_specs=[vmem, vmem, vmem],
         out_specs=(hbm, hbm, hbm),
         scratch_shapes=[
             pltpu.VMEM((1, CD, RD), F32),
@@ -579,7 +594,7 @@
         ],
         compiler_params=pltpu.CompilerParams(vmem_limit_bytes=8 * 1024 * 1024),
         name="finish",
-    )(field, stats)
+    )(field, rows, sums)
 
 
 def solution(mesh):

time: 49.7 us -> 45.8 us (0.922)
  Pallas kernels: 49 us -> 45.1 us
    pallas_call x2, Pallas kernels: 49 us -> 45.1 us  [the longest x1 44.2 us: body(): pl.pallas_call(kernel, out_shape=(jax.ShapeDtypeStruct((1, CD, RD, ND), B...]
where the time goes in v6:
time: 45.8 us; the launch traced here: 45.7 us
  Pallas kernels  45.1 us (98%)
  between operations  0.64 us (1%)
    pallas_call x1, Pallas kernels, body(): pl.pallas_call(kernel, out_shape=(jax.ShapeDtypeStruct((1, CD, RD, ND), B...  44.2 us

profile of v6, /device:TPU:1, one launch (start us, length us, event | category | flops | bytes accessed | tf_op | source)
XLA Modules:
  0.0 45.7 jit_solution(4729799654474988706)
XLA Ops:
  0.6 44.2 %spectral_layer.1 = (bf16[1,32,96,128]{3,2,1,0:T(8,128)(2,1)S(1)}, f32[8,16,128]{2,1,0:T(8,128)S(1)}, f32[32,2,128]{2,1,0:T(2,128)S(1)}) custom-call(bf16[1,32,96,128]{3,2,1,0:T(8,128)(2,1)} %state.1, bf16[1024,256]{1,0:T(8,128)(2,1)} %constant.10.clone.etab, bf16[4,192,192]{2,1,0:T(8,128)(2,1)} %constant.11.clone.qtab, ...), custom_call_target="tpu_custom_call" | custom-call | tf_op jit(solution)/shard_map/spectral_layer/pallas_call | solution.py:530
  44.8 0.9 %finish.1 = (bf16[1,32,96,128]{3,2,1,0:T(8,128)(2,1)}, f32[1,32,96]{2,1,0:T(8,128)}, f32[32]{0:T(128)}) custom-call(bf16[1,32,96,128]{3,2,1,0:T(8,128)(2,1)S(1)} %get-tuple-element.6.refs_0_, f32[8,16,128]{2,1,0:T(8,128)S(1)} %get-tuple-element.7.refs_1_, f32[32,2,128]{2,1,0:T(2,128)S(1)} %get-tuple-element.8.refs_2_), custom_call_target="tpu_custom_call" | custom-call | tf_op jit(solution)/shard_map/finish/pallas_call | solution.py:581

commit v7 on v6

--- a/solution.py
+++ b/solution.py
@@ -130,14 +130,11 @@
     bcol,
     xin,
     ss,
-    sa,
-    sb,
+    sp,
     sc,
-    ra,
-    rb,
+    rp,
     rc,
-    xa,
-    xb,
+    xp,
     xc,
     ma,
     mb,
@@ -147,7 +144,6 @@
     bc,
     fs,
     zacc,
-    eacc,
     zmsg,
     emsg,
     load_sem,
@@ -269,8 +265,8 @@
         p0, p1 = jnp.where(high, up_r, t[0]), jnp.where(high, half_r, t[1])
         p2, p3 = jnp.where(high, up_i, t[3]), jnp.where(high, half_i, t[4])
         p4 = jnp.where(low, half_r, jnp.where(second, up_i, 0.0))
-        sa[slot] = jnp.concatenate([p0, p2], axis=1).astype(BF)
-        sb[slot] = jnp.concatenate([p1, p3], axis=1).astype(BF)
+        for i, p in enumerate((p0, p2, p1, p3)):
+            sp[i, slot] = p.astype(BF)
         sc[slot] = (p4[0:8] + pltpu.roll(p4[8:16], 64, 1)).astype(BF)
 
     def copy2(src_ref, dst_ref, part, peer):
@@ -285,18 +281,21 @@
         )
 
     scope("pack")
-    for i in range(0, len(PEERS), 8):
-        for peer in PEERS[i : i + 8]:
+    done = 0
+    for size in (3, 6, 8, 8, 6):
+        for peer in PEERS[done : done + size]:
             pack(plane(peer)[1])
-        for peer in PEERS[i : i + 8]:
-            copy2(sa, ra, 0, peer).start()
+        for peer in PEERS[done : done + size]:
+            copy2(sp.at[0], rp.at[0], 0, peer).start()
+        done += size
+    for i in range(1, 4):
+        for peer in PEERS:
+            copy2(sp.at[i], rp.at[i], i, peer).start()
     for peer in PEERS:
-        copy2(sb, rb, 1, peer).start()
-    for peer in PEERS:
-        copy2(sc, rc, 2, peer).start()
+        copy2(sc, rc, 4, peer).start()
     pack(me)
-    ra[me] = sa[me]
-    rb[me] = sb[me]
+    for i in range(4):
+        rp[i, me] = sp[i, me]
     rc[me] = sc[me]
     bias_r = jnp.broadcast_to(turned[:, 0:1], (256, 128))
     bias_i = jnp.broadcast_to(turned[:, 1:2], (256, 128))
@@ -309,7 +308,8 @@
         some = ref.at[pl.ds(0, NVAR - 1)]
         return pltpu.make_async_copy(some, some, sem)
 
-    for part, (got, every) in enumerate(((ra, xa), (rb, xb), (rc, xc))):
+    stages = [(sp.at[i], rp.at[i], xp.at[i]) for i in range(4)] + [(sc, rc, xc)]
+    for part, (_, got, every) in enumerate(stages):
         scope(f"wait2_{part}")
         whole_at(got, r2.at[part])
         scope(f"sum_{part}")
@@ -342,15 +342,16 @@
         gr, gi = g[:half], g[half:]
         return (jnp.where(which, gr - pltpu.roll(gi, 96, 1), gr + pltpu.roll(gi, 32, 1)),)
 
-    def mixed(every, part):
-        others(every, r3.at[part]).wait()
-        scope(f"mix_{part}")
-        if every is xc:
+    def mixed(*parts):
+        for part in parts:
+            others(stages[part][2], r3.at[part]).wait()
+        scope(f"mix_{parts[0]}")
+        if len(parts) == 1:
             folded = xc[...].astype(F32).reshape(2 * NVAR, 8, 128)
             beside = pltpu.roll(folded, 64, 2)
             rows = jnp.stack([folded, beside], axis=1).reshape(256, 128).astype(BF)
         else:
-            rows = every[...].reshape(256, -1)
+            rows = jnp.concatenate([xp[part].reshape(256, 128) for part in parts], axis=1)
         g = jnp.dot(wiv[...].reshape(512, 256), rows, preferred_element_type=F32)
         tiles = combined(g, 256)
         which = lax.broadcasted_iota(jnp.int32, (256, 128), 1) < 32
@@ -376,13 +377,13 @@
             copy4(src_ref, dst_ref, part, peer).start()
         dst_ref[me] = src_ref[core]
 
-    ma[...] = jnp.concatenate(mixed(xa, 0), axis=1).astype(BF).reshape(2, CH, 256)
+    ma[...] = jnp.concatenate(mixed(0, 1), axis=1).astype(BF).reshape(2, CH, 256)
     spread(0, ma, ba)
     scope("wait3_1")
-    mb[...] = jnp.concatenate(mixed(xb, 1), axis=1).astype(BF).reshape(2, CH, 256)
+    mb[...] = jnp.concatenate(mixed(2, 3), axis=1).astype(BF).reshape(2, CH, 256)
     spread(1, mb, bb)
     scope("wait3_2")
-    (last,) = mixed(xc, 2)
+    (last,) = mixed(4)
     last = jnp.where(lax.broadcasted_iota(jnp.int32, (CD, 128), 1) < 64, last, 0.0).reshape(2, 2, 8, 128)
     mc[...] = (last[:, 0] + pltpu.roll(last[:, 1], 64, 2)).astype(BF)
     spread(2, mc, bc)
@@ -390,14 +391,25 @@
     def put(owner, i, tile):
         ss[pl.ds(owner * 6 + i, CH, stride=PITCH), :] = tile
 
-    for part, (got, i) in enumerate(((ba, 0), (bb, 1))):
-        scope(f"wait4_{part}")
-        whole_at(got, r4.at[part])
-        scope(f"unpack_{part}")
-        for o in range(PLANE):
-            tiles = got[o].astype(F32)
-            put(o, i, tiles[:, 0:128])
-            put(o, i + 3, tiles[:, 128:256])
+    def have(owner, i):
+        return ss[pl.ds(owner * 6 + i, CH, stride=PITCH), :]
+
+    scope("wait4_0")
+    whole_at(ba, r4.at[0])
+    scope("unpack_0")
+    for o in range(PLANE):
+        tiles = ba[o].astype(F32)
+        for i, tile in ((0, tiles[:, 0:128]), (3, tiles[:, 128:256])):
+            put(o, i, tile)
+            put(o, i + 2, pltpu.roll(tile, 32, 1))
+    scope("wait4_1")
+    whole_at(bb, r4.at[1])
+    scope("unpack_1")
+    for o in range(PLANE):
+        tiles = bb[o].astype(F32)
+        for i, tile in ((1, tiles[:, 0:128]), (4, tiles[:, 128:256])):
+            put(o, i, tile)
+            put(o, i + 1, jnp.where(low, have(o, i + 1), pltpu.roll(tile, 64, 1)))
     scope("wait4_2")
     for load in loads[8:]:
         load.wait()
@@ -405,13 +417,13 @@
     scope("unpack_2")
     mid = lane < 64
     for o in range(PLANE):
-        one, two, folded = ba[o].astype(F32), bb[o].astype(F32), bc[o].astype(F32)
-        end = jnp.concatenate([folded, pltpu.roll(folded, 64, 1)], axis=0)
-        for i, cols, shift in ((2, slice(0, 128), 64), (5, slice(128, 256), 32)):
-            start = jnp.where(low, pltpu.roll(one[:, cols], 32, 1), pltpu.roll(two[:, cols], 64, 1))
-            put(o, i, jnp.where(mid, start, pltpu.roll(end, shift, 1)))
+        folded = bc[o].astype(F32)
+        turned_by = [pltpu.roll(folded, shift, 1) for shift in (64, 32, 96)]
+        put(o, 2, jnp.where(mid, have(o, 2), jnp.concatenate([turned_by[0], folded], axis=0)))
+        put(o, 5, jnp.where(mid, have(o, 5), jnp.concatenate(turned_by[1:], axis=0)))
 
     column = lax.broadcasted_iota(jnp.int32, (RD, 128), 1)
+    powers = jnp.zeros((8, 128), F32)
     for c in range(0, CH, 2):
         if c % PIECE == 0:
             scope(f"gelu{c}")
@@ -433,7 +445,8 @@
             zacc[0:RD, :] += jnp.where(column == at, total, 0.0)
             part = square[i * RD : (i + 1) * RD]
             part = (part[:, 0:128] + part[:, 128:256]) * gv[...]
-            eacc[at] = jnp.sum(part.reshape(RD // 8, 8, 128), axis=0)
+            part = jnp.sum(jnp.sum(part.reshape(RD // 8, 8, 128), axis=0), axis=1, keepdims=True)
+            powers += jnp.where(column[0:8] == core * CH + at, part, 0.0)
         if (c + 2) % PIECE == 0:
             first = c + 2 - PIECE
             pltpu.make_async_remote_copy(
@@ -447,12 +460,7 @@
 
     scope("stats")
     zmsg[...] = jnp.transpose(zacc[...])[0:CH]
-    ones = jnp.ones((8, 128), F32)
-    highest = dict(precision=lax.Precision.HIGHEST, preferred_element_type=F32)
-    flat = lax.dot_general(ones, eacc[...].reshape(CH * 8, 128), (((1,), (1,)), ((), ())), **highest)
-    channel = lax.div(lax.broadcasted_iota(jnp.int32, (128, 128), 0), 8) + core * CH
-    pick = jnp.where(channel == lax.broadcasted_iota(jnp.int32, (128, 128), 1), 1.0, 0.0)
-    emsg[...] = jnp.dot(flat, pick, **highest)[0:2]
+    emsg[...] = jnp.broadcast_to(jnp.sum(powers, axis=0, keepdims=True), (2, 128))
 
     def copy6(peer):
         to, slot = plane(peer)
@@ -486,9 +494,10 @@
     erec[me] = emsg[...]
     scope("wait5")
     pltpu.make_async_copy(xin, xin, s1.at[0]).wait()
-    for part, (sent, every, spreads) in enumerate(((sa, xa, ba), (sb, xb, bb), (sc, xc, bc))):
+    for part, (sent, _, every) in enumerate(stages):
         whole_at(sent, s2.at[part])
         others(every, s3.at[part]).wait()
+    for part, spreads in enumerate((ba, bb, bc)):
         whole_at(spreads, s4.at[part])
     half = fs.at[pl.ds(0, CH)]
     pltpu.make_async_copy(half, half, s5.at[0]).wait()
@@ -548,14 +557,11 @@
             pltpu.VMEM((128, 256), F32),
             pltpu.VMEM((CH, RD, ND), BF),
             pltpu.VMEM((CH * PITCH, 128), F32),
-            pltpu.VMEM((PLANE, CH, 256), BF),
-            pltpu.VMEM((PLANE, CH, 256), BF),
+            pltpu.VMEM((4, PLANE, CH, 128), BF),
             pltpu.VMEM((PLANE, 8, 128), BF),
-            pltpu.VMEM((PLANE, CH, 256), BF),
-            pltpu.VMEM((PLANE, CH, 256), BF),
+            pltpu.VMEM((4, PLANE, CH, 128), BF),
             pltpu.VMEM((PLANE, 8, 128), BF),
-            pltpu.VMEM((NVAR, CD, 256), BF),
-            pltpu.VMEM((NVAR, CD, 256), BF),
+            pltpu.VMEM((4, NVAR, CD, 128), BF),
             pltpu.VMEM((NVAR, CH, 128), BF),
             pltpu.VMEM((2, CH, 256), BF),
             pltpu.VMEM((2, CH, 256), BF),
@@ -565,12 +571,11 @@
             pltpu.VMEM((PLANE, 8, 128), BF),
             pltpu.VMEM((CH, RD, ND), BF),
             pltpu.VMEM((128, 128), F32),
-            pltpu.VMEM((CH, 8, 128), F32),
             pltpu.VMEM((CH, 128), F32),
             pltpu.VMEM((2, 128), F32),
             dma((12,)),
         ]
-        + [dma((1,)), dma((PIECES,)), dma((3,)), dma((3,)), dma((3,)), dma((3,))]
+        + [dma((1,)), dma((PIECES,)), dma((5,)), dma((5,)), dma((5,)), dma((5,))]
         + [dma((3,)), dma((3,))]
         + [dma((1,)), dma((1,))] * 3,
         compiler_params=pltpu.CompilerParams(

time: 45.8 us -> 43.5 us (0.950)
  Pallas kernels: 45.1 us -> 42.8 us
    pallas_call x1, Pallas kernels: 44.2 us -> 41.9 us  [body(): pl.pallas_call(kernel, out_shape=(jax.ShapeDtypeStruct((1, CD, RD, ND), B...]
where the time goes in v7:
time: 43.5 us; the launch traced here: 43.4 us
  Pallas kernels  42.8 us (98%)
  between operations  0.64 us (1%)
    pallas_call x1, Pallas kernels, body(): pl.pallas_call(kernel, out_shape=(jax.ShapeDtypeStruct((1, CD, RD, ND), B...  41.9 us
    pallas_call x1, Pallas kernels, body(): pl.pallas_call(lambda *refs: finish(total_area, *refs), out_shape=(jax.Sh...  0.91 us

profile of v7, /device:TPU:1, one launch (start us, length us, event | category | flops | bytes accessed | tf_op | source)
XLA Modules:
  0.0 43.4 jit_solution(719137608048531656)
XLA Ops:
  0.6 41.9 %spectral_layer.1 = (bf16[1,32,96,128]{3,2,1,0:T(8,128)(2,1)S(1)}, f32[8,16,128]{2,1,0:T(8,128)S(1)}, f32[32,2,128]{2,1,0:T(2,128)S(1)}) custom-call(bf16[1,32,96,128]{3,2,1,0:T(8,128)(2,1)} %state.1, bf16[1024,256]{1,0:T(8,128)(2,1)} %constant.10.clone.etab, bf16[4,192,192]{2,1,0:T(8,128)(2,1)} %constant.11.clone.qtab, ...), custom_call_target="tpu_custom_call" | custom-call | tf_op jit(solution)/shard_map/spectral_layer/pallas_call | solution.py:539
  42.5 0.9 %finish.1 = (bf16[1,32,96,128]{3,2,1,0:T(8,128)(2,1)}, f32[1,32,96]{2,1,0:T(8,128)}, f32[32]{0:T(128)}) custom-call(bf16[1,32,96,128]{3,2,1,0:T(8,128)(2,1)S(1)} %get-tuple-element.6.refs_0_, f32[8,16,128]{2,1,0:T(8,128)S(1)} %get-tuple-element.7.refs_1_, f32[32,2,128]{2,1,0:T(2,128)S(1)} %get-tuple-element.8.refs_2_), custom_call_target="tpu_custom_call" | custom-call | tf_op jit(solution)/shard_map/finish/pallas_call | solution.py:586
